TPU v7x, 32 devices: a whole 2x2x4 slice. The times are simulated.
32 devices in a mesh: inner: 2 (over y), outer: 4 (over z), head: 4 (over x, core).
Axes of the slice: x: 2, y: 2, z: 4, core: 2. Of those that a mesh axis runs over, the one named last changes fastest.
Arguments:
- queries: bfloat16 [2048, 64, 128], P(('inner', 'outer', 'head')), may hold values from -6 to 6
- key_vector_rows: bfloat16 [2048, 8, 128], P(('inner', 'outer'), 'head'), may hold values from -6 to 6
- value_vector_rows: bfloat16 [2048, 8, 128], P(('inner', 'outer'), 'head'), may hold values from -6 to 6
- grad_out: bfloat16 [2048, 64, 128], P(('inner', 'outer', 'head')), may hold values from -24 to 24
Outputs:
- query_grads: bfloat16 [2048, 64, 128], P(('inner', 'outer', 'head'))
- key_gradient_rows: bfloat16 [2048, 8, 128], P(('inner', 'outer'), 'head')
- value_gradient_rows: bfloat16 [2048, 8, 128], P(('inner', 'outer'), 'head')
All inputs are finite; a program needn't handle non-finite values.
Results may differ from a plain program's by a relative error of at most 0.012.
Values may be sent and summed in bfloat16 or wider, within the bound.
No kernel may reach another device: no remote copies, remote signals or barrier semaphores. Data moves between devices by JAX's collectives and lax.ppermute only.
A program may use at most 64 MiB of HBM per device.

v0:
```python
import functools
import math

import jax
import jax.numpy as jnp
from jax import lax
from jax.experimental import pallas as pl
from jax.experimental.pallas import tpu as pltpu
from jax.sharding import PartitionSpec as P


NT = (((1,), (1,)), ((), ()))
SEQ = ("inner", "outer")
NEVER = 1e30
BLOCK = 256
VMEM = pl.BlockSpec(memory_space=pltpu.VMEM)
HBM = pl.BlockSpec(memory_space=pltpu.HBM)


def shifted(value, by):
    peers = lax.axis_size(SEQ)
    pairs = [(i, (i + by) % peers) for i in range(peers)]
    return lax.ppermute(value, SEQ, pairs)


def swapped(value, distance):
    peers = lax.axis_size("head")
    return lax.ppermute(value, "head", [(i, i ^ distance) for i in range(peers)])


def in_hbm(value):
    return pltpu.with_memory_space_constraint(value, pltpu.HBM)


def pack_copies(parts, sources, outs, sem, kv_heads):
    me = lax.axis_index("head")
    copies = []
    for out, part in zip(outs, parts):
        for n, (kv, distance) in enumerate(part):
            place = (me ^ distance) * kv_heads + kv
            for which, source in enumerate(sources):
                copies.append(
                    pltpu.make_async_copy(source.at[:, place], out.at[n, which], sem.at[len(copies)])
                )
    return copies


def pack_kernel(parts, kv_heads, q_ref, do_ref, *refs):
    copies = pack_copies(parts, (q_ref, do_ref), refs[:-1], refs[-1], kv_heads)
    for copy in copies:
        copy.start()
    for copy in copies:
        copy.wait()


def first_kernel(parts, kv_heads, key_ref, value_ref, q_ref, do_ref, *refs):
    own_refs, outs = refs[:kv_heads], refs[kv_heads:-4]
    narrow, wide, own_sem, sem = refs[-4:]
    loads = [
        pltpu.make_async_copy(source, narrow.at[which], own_sem.at[which])
        for which, source in enumerate((key_ref, value_ref))
    ]
    copies = pack_copies(parts, (q_ref, do_ref), outs, sem, kv_heads)
    for copy in loads + copies:
        copy.start()
    tok_rows = own_refs[0].shape[1]
    for which, load in enumerate(loads):
        load.wait()
        wide[which] = narrow[which].astype(jnp.float32)
        for kv in range(kv_heads):
            rows = wide[which, pl.ds(kv, tok_rows, stride=kv_heads), :]
            own_refs[kv][which] = rows.astype(own_refs[kv].dtype)
    for copy in copies:
        copy.wait()


def pack(queries, grad_out, parts, kv_heads):
    part_rows, _, group, width = queries.shape
    return pl.pallas_call(
        functools.partial(pack_kernel, parts, kv_heads),
        in_specs=[HBM, HBM],
        out_specs=[VMEM] * len(parts),
        out_shape=[
            pltpu.VMEM((len(part), 2, part_rows, group, width), queries.dtype) for part in parts
        ],
        scratch_shapes=[pltpu.SemaphoreType.DMA((2 * sum(len(part) for part in parts),))],
        compiler_params=pltpu.CompilerParams(vmem_limit_bytes=16 * 2**20),
        name="pack",
    )(in_hbm(queries), in_hbm(grad_out))


def pack_first(keys, values, queries, grad_out, parts):
    tok_rows, kv_heads, width = keys.shape
    part_rows, _, group, _ = queries.shape
    outs = pl.pallas_call(
        functools.partial(first_kernel, parts, kv_heads),
        in_specs=[HBM] * 4,
        out_specs=[VMEM] * (len(parts) + kv_heads),
        out_shape=[pltpu.VMEM((2, tok_rows, width), keys.dtype)] * kv_heads
        + [pltpu.VMEM((len(part), 2, part_rows, group, width), queries.dtype) for part in parts],
        scratch_shapes=[
            pltpu.VMEM((2, tok_rows * kv_heads, width), keys.dtype),
            pltpu.VMEM((2, tok_rows * kv_heads, width), jnp.float32),
            pltpu.SemaphoreType.DMA((2,)),
            pltpu.SemaphoreType.DMA((2 * sum(len(part) for part in parts),)),
        ],
        compiler_params=pltpu.CompilerParams(vmem_limit_bytes=16 * 2**20),
        name="first",
    )(
        in_hbm(keys.reshape(tok_rows * kv_heads, width)),
        in_hbm(values.reshape(tok_rows * kv_heads, width)),
        in_hbm(queries),
        in_hbm(grad_out),
    )
    return outs[:kv_heads], outs[kv_heads:]


def finish_kernel(parts, heads, *refs):
    values, totals = refs[: len(parts)], refs[len(parts) : len(parts) + 3 * heads]
    dq_ref, dk_ref, dv_ref, wide, narrow, sem = refs[len(parts) + 3 * heads :]
    me = lax.axis_index("head")
    copies = []
    for value, part in zip(values, parts):
        for n, (kv, distance) in enumerate(part):
            place = (me ^ distance) * heads + kv
            copies.append(
                pltpu.make_async_copy(value.at[n], dq_ref.at[:, place], sem.at[len(copies)])
            )
    for copy in copies:
        copy.start()
    tok_rows = totals[0].shape[1]
    for which, out in enumerate((dk_ref, dv_ref)):
        for kv in range(heads):
            own, far, near = totals[3 * kv : 3 * kv + 3]
            total = own[which] + far[which].astype(jnp.float32) + near[which].astype(jnp.float32)
            wide[which, pl.ds(kv, tok_rows, stride=heads), :] = total
        narrow[which] = wide[which].astype(narrow.dtype)
        copies.append(pltpu.make_async_copy(narrow.at[which], out, sem.at[len(copies)]))
        copies[-1].start()
    for copy in copies:
        copy.wait()


def finish(values, parts, totals):
    _, part_rows, group, width = values[0].shape
    heads = len(totals)
    tok_rows = totals[0][0].shape[1]
    places = sum(len(part) for part in parts)
    dq, dk, dv = pl.pallas_call(
        functools.partial(finish_kernel, parts, heads),
        in_specs=[VMEM] * (len(values) + 3 * heads),
        out_specs=[HBM] * 3,
        out_shape=[
            jax.ShapeDtypeStruct((part_rows, places, group, width), jnp.bfloat16),
            jax.ShapeDtypeStruct((tok_rows * heads, width), jnp.bfloat16),
            jax.ShapeDtypeStruct((tok_rows * heads, width), jnp.bfloat16),
        ],
        scratch_shapes=[
            pltpu.VMEM((2, tok_rows * heads, width), jnp.float32),
            pltpu.VMEM((2, tok_rows * heads, width), jnp.bfloat16),
            pltpu.SemaphoreType.DMA((places + 2,)),
        ],
        compiler_params=pltpu.CompilerParams(vmem_limit_bytes=16 * 2**20),
        name="finish",
    )(*values, *(term for total in totals for term in total))
    return (
        dq.reshape(part_rows, places * group, width),
        dk.reshape(tok_rows, heads, width),
        dv.reshape(tok_rows, heads, width),
    )


def grads_kernel(where, distances, fresh, last, *refs):
    count = len(distances)
    pair_refs, windows = refs[:count], refs[count : count + 3]
    spent = count + 3 + (0 if fresh else 1)
    old_ref = None if fresh else refs[count + 3]
    dq_refs = refs[spent : spent + count]
    sum_refs = refs[spent + count : -2]
    acc, kt = refs[-2:]
    _, part_rows, group, width = pair_refs[0].shape[1:]
    rows = part_rows * group
    block_rows = min(rows, BLOCK)
    scale = width ** (-0.5)
    to_exp2 = scale * math.log2(math.e)
    me = lax.axis_index("head")
    block = lax.axis_index(SEQ)
    bias = (
        jnp.where(block < 2, NEVER, 0.0).astype(jnp.float32),
        jnp.where(block < 1, NEVER, 0.0).astype(jnp.float32),
        0.0,
    )
    for j, window in enumerate(windows):
        kt[j] = window[0].T
    tokens = block_rows // group
    pieces = [(n, t) for n in range(count) for t in range(0, part_rows, tokens)]

    def part(piece, which):
        n, t = piece
        return pair_refs[n][where[n], which, t : t + tokens].reshape(block_rows, width)

    def scored(piece):
        n, t = piece
        q = part(piece, 0)
        first = (me ^ distances[n]) * rows + t * group
        scores, tops = [], []
        for j, window in enumerate(windows):
            s = lax.dot_general(window[0], q, NT, preferred_element_type=jnp.float32)
            if j == 2:
                token = (lax.broadcasted_iota(jnp.int32, (1, block_rows), 1) + first) // group
                key = lax.broadcasted_iota(jnp.int32, s.shape, 0)
                s = jnp.where(key <= token, s, -jnp.inf)
            scores.append(s)
            tops.append(jnp.max(s, axis=0, keepdims=True) - bias[j])
        return scores, jnp.maximum(jnp.maximum(tops[0], tops[1]), tops[2]) * to_exp2

    ahead = scored(pieces[0])
    for step, piece in enumerate(pieces):
        scores, top = ahead
        q, do = part(piece, 0), part(piece, 1)
        weights, dprobs, total, dtotal = [], [], 0.0, 0.0
        for j, window in enumerate(windows):
            e = jnp.exp2(scores[j] * to_exp2 - (top + bias[j]))
            dp = lax.dot_general(window[1], do, NT, preferred_element_type=jnp.float32)
            total = total + jnp.sum(e, axis=0, keepdims=True)
            dtotal = dtotal + jnp.sum(e * dp, axis=0, keepdims=True)
            weights.append(e)
            dprobs.append(dp)
        if step + 1 < len(pieces):
            ahead = scored(pieces[step + 1])
        inverse = 1.0 / total
        delta = dtotal * inverse
        dqt = 0.0
        for j in range(3):
            p = weights[j] * inverse
            ds = (p * (dprobs[j] - delta)).astype(jnp.bfloat16)
            dv = jnp.dot(p.astype(jnp.bfloat16), do, preferred_element_type=jnp.float32)
            dk = jnp.dot(ds, q, preferred_element_type=jnp.float32)
            if step == 0:
                if not fresh:
                    dk, dv = old_ref[j, 0] + dk, old_ref[j, 1] + dv
                acc[j, 0], acc[j, 1] = dk, dv
            else:
                acc[j, 0] += dk
                acc[j, 1] += dv
            dqt = dqt + jnp.dot(kt[j], ds, preferred_element_type=jnp.float32)
        n, t = piece
        dq = (dqt * scale).T.astype(jnp.bfloat16)
        dq_refs[n][0, t : t + tokens] = dq.reshape(tokens, group, width)
    if last:
        for j, out in enumerate(sum_refs):
            out[0] = (acc[j, 0] * scale).astype(out.dtype)
            out[1] = acc[j, 1].astype(out.dtype)
    else:
        sum_refs[0][...] = acc[...]


def group_grads(pairs, where, distances, window, sums, last):
    count = len(pairs)
    _, _, part_rows, group, width = pairs[0].shape
    tok_rows = window[2].shape[1]
    rows = part_rows * group
    cells = count * rows * 3 * tok_rows
    shape = (2, tok_rows, width)
    if last:
        kinds = [pltpu.VMEM(shape, jnp.bfloat16)] * 2 + [pltpu.VMEM(shape, jnp.float32)]
    else:
        kinds = [pltpu.VMEM((3, *shape), jnp.float32)]
    old = [] if sums is None else [sums]
    outs = pl.pallas_call(
        functools.partial(grads_kernel, where, distances, sums is None, last),
        in_specs=[VMEM] * (count + 3 + len(old)),
        out_specs=[VMEM] * (count + len(kinds)),
        out_shape=[pltpu.VMEM((1, part_rows, group, width), jnp.bfloat16)] * count + kinds,
        scratch_shapes=[
            pltpu.VMEM((3, *shape), jnp.float32),
            pltpu.VMEM((3, width, tok_rows), jnp.bfloat16),
        ],
        compiler_params=pltpu.CompilerParams(vmem_limit_bytes=32 * 2**20),
        cost_estimate=pl.CostEstimate(
            flops=10 * cells * width, bytes_accessed=6 * count * rows * width, transcendentals=cells
        ),
        name="grads",
    )(*pairs, *window, *old)
    return outs[:count], outs[count:]


def shards(queries, key_vector_rows, value_vector_rows, grad_out):
    part_rows, heads, width = queries.shape
    kv_heads = key_vector_rows.shape[1]
    peers = lax.axis_size("head")
    group = heads // (peers * kv_heads)
    places = peers * kv_heads
    queries = queries.reshape(part_rows, places, group, width)
    grad_out = grad_out.reshape(part_rows, places, group, width)
    far_cores = list(range(2, peers))
    all_kv = list(range(kv_heads))

    own, first = pack_first(
        key_vector_rows, value_vector_rows, queries, grad_out, [[(0, d)] for d in far_cores]
    )
    rest = pack(
        queries,
        grad_out,
        [[(kv, 0) for kv in all_kv], [(kv, 1) for kv in all_kv]]
        + [[(kv, d)] for kv in all_kv[1:] for d in far_cores],
        kv_heads,
    )
    sent = [first] + [rest[2 + n * len(far_cores) :][: len(far_cores)] for n in range(kv_heads - 1)]
    crossed, windows = [], []
    for kv in all_kv:
        values = []
        for value, d in zip(sent[kv], far_cores):
            values.append(swapped(value, d))
        crossed.append(values)
        far = shifted(own[kv], 2)
        near = shifted(own[kv], 1)
        windows.append((far, near, own[kv]))
    here = rest[0]
    partner = swapped(rest[1], 1)
    dq, totals = {}, []
    for kv in all_kv:
        final = kv == all_kv[-1]
        turns = [[0, 1]] + [[d] for d in far_cores]
        sums = None
        for turn in turns:
            values = {0: here, 1: partner, **dict(zip(far_cores, crossed[kv]))}
            made, sums = group_grads(
                [values[d] for d in turn],
                [kv if d < 2 else 0 for d in turn],
                turn,
                windows[kv],
                None if sums is None else sums[0],
                turn is turns[-1],
            )
            for d, value in zip(turn, made):
                if d >= 2:
                    value = swapped(value, d)
                dq[kv, d] = value
        dfar = shifted(sums[0], -2)
        dnear = shifted(sums[1], -1)
        totals.append((sums[2], dfar, dnear))
    dq_partner = swapped(jnp.concatenate([dq[kv, 1] for kv in all_kv], axis=0), 1)
    parts = [[(kv, 0)] for kv in all_kv] + [[(kv, 1) for kv in all_kv]]
    parts += [[(kv, d)] for kv in all_kv for d in far_cores]
    values = [dq[part[0]] if len(part) == 1 else dq_partner for part in parts]
    return finish(values, parts, totals)


def solution(mesh):
    return jax.shard_map(
        shards,
        mesh=mesh,
        in_specs=(
            P(("inner", "outer", "head"), None, None),
            P(("inner", "outer"), "head", None),
            P(("inner", "outer"), "head", None),
            P(("inner", "outer", "head"), None, None),
        ),
        out_specs=(
            P(("inner", "outer", "head"), None, None),
            P(("inner", "outer"), "head", None),
            P(("inner", "outer"), "head", None),
        ),
        check_vma=False,
    )
```

profile of v0, /device:TPU:0, one launch (start us, length us, event | category | flops | bytes accessed | tf_op | source)
XLA Modules:
  0.0 56.8 jit_solution(61197713772061001)
XLA Ops:
  0.6 1.6 %pack.1 = (bf16[2,2,64,8,128]{4,3,2,1,0:T(8,128)(2,1)S(1)}, bf16[2,2,64,8,128]{4,3,2,1,0:T(8,128)(2,1)S(1)}, bf16[1,2,64,8,128]{4,3,2,1,0:T(8,128)(2,1)S(1)}, bf16[1,2,64,8,128]{4,3,2,1,0:T(8,128)(2,1)S(1)}) custom-call(bf16[64,8,8,128]{3,2,1,0:T(8,128)(2,1)} %bitcast.7, bf16[64,8,8,128]{3,2,1,0:T(8,128)(2,1)} %bitcast.9), custom_call_target="tpu_custom_call" | custom-call | tf_op jit(solution)/shard_map/pack/pallas_call | solution.py:79
  2.2 0.6 collective-permute-start
  2.8 2.6 %collective-permute-start.10 = (bf16[1,2,64,8,128]{4,3,2,1,0:T(8,128)(2,1)S(1)}, bf16[1,2,64,8,128]{4,3,2,1,0:T(8,128)(2,1)S(1)}, u32[]{:S(2)}, u32[]{:S(2)}) collective-permute-start(bf16[1,2,64,8,128]{4,3,2,1,0:T(8,128)(2,1)S(1)} %get-tuple-element.46), channel_id=1, source_target_pairs={{0,2},{1,3},{2,0},{3,1},{4,6},{5,7},{6,4},{7,5},{8,10},{9,11},{10,... | collective-permute-start | bytes 786440 | tf_op jit(solution)/shard_map/ppermute | solution.py:28
  5.3 1.3 %first.1 = (bf16[2,256,128]{2,1,0:T(8,128)(2,1)S(1)}, bf16[2,256,128]{2,1,0:T(8,128)(2,1)S(1)}, bf16[1,2,64,8,128]{4,3,2,1,0:T(8,128)(2,1)S(1)}, bf16[1,2,64,8,128]{4,3,2,1,0:T(8,128)(2,1)S(1)}) custom-call(bf16[512,128]{1,0:T(8,128)(2,1)} %bitcast.11, bf16[512,128]{1,0:T(8,128)(2,1)} %bitcast.12, bf16[64,8,8,128]{3,2,1,0:T(8,128)(2,1)} %bitcast.8, ...), custom_call_target="tpu_custom_call" | custom-call | tf_op jit(solution)/shard_map/first/pallas_call | solution.py:95
  6.6 2.6 %collective-permute-start.3 = (bf16[2,256,128]{2,1,0:T(8,128)(2,1)S(1)}, bf16[2,256,128]{2,1,0:T(8,128)(2,1)S(1)}, u32[]{:S(2)}, u32[]{:S(2)}) collective-permute-start(bf16[2,256,128]{2,1,0:T(8,128)(2,1)S(1)} %get-tuple-element.36.refs_4_.refs_3_), channel_id=1, source_target_pairs={{0,8},{4,12},{8,16},{12,20},{16,24},{20,28},{24,0},{28,4},{1,9},{5... | collective-permute-start | bytes 393224 | tf_op jit(solution)/shard_map/ppermute | solution.py:23
  9.3 1.6 %collective-permute-start.4 = (bf16[2,256,128]{2,1,0:T(8,128)(2,1)S(1)}, bf16[2,256,128]{2,1,0:T(8,128)(2,1)S(1)}, u32[]{:S(2)}, u32[]{:S(2)}) collective-permute-start(bf16[2,256,128]{2,1,0:T(8,128)(2,1)S(1)} %get-tuple-element.36.refs_4_.refs_3_), channel_id=1, source_target_pairs={{0,4},{4,8},{8,12},{12,16},{16,20},{20,24},{24,28},{28,0},{1,5},{5... | collective-permute-start | bytes 393224 | tf_op jit(solution)/shard_map/ppermute | solution.py:23
  10.8 0.0 collective-permute-start.12
  10.8 8.8 %collective-permute-done.3.refs_2_.refs_1_ = bf16[2,256,128]{2,1,0:T(8,128)(2,1)S(1)} collective-permute-done((bf16[2,256,128]{2,1,0:T(8,128)(2,1)S(1)}, bf16[2,256,128]{2,1,0:T(8,128)(2,1)S(1)}, u32[]{:S(2)}, u32[]{:S(2)}) %collective-permute-start.3) | collective-permute-done | bytes 131104 | tf_op jit(solution)/shard_map/ppermute | solution.py:23
  19.6 0.0 collective-permute-start.1
  19.7 0.0 collective-permute-done.4.refs_3_.refs_2_
  19.7 0.5 collective-permute-start.2
  20.1 0.0 collective-permute-done.10.refs_0_
  20.1 0.5 collective-permute-start.6
  20.6 0.0 collective-permute-done.refs_1_
  20.6 0.2 collective-permute-start.8
  20.9 2.9 %grads.7 = (bf16[1,64,8,128]{3,2,1,0:T(8,128)(2,1)S(1)}, bf16[1,64,8,128]{3,2,1,0:T(8,128)(2,1)S(1)}, f32[3,2,256,128]{3,2,1,0:T(8,128)S(1)}) custom-call(bf16[2,2,64,8,128]{4,3,2,1,0:T(8,128)(2,1)S(1)} %get-tuple-element.32.refs_0_, bf16[2,2,64,8,128]{4,3,2,1,0:T(8,128)(2,1)S(1)} %collective-permute-done.refs_1_, ...), custom_call_target="tpu_custom_call" | custom-call | flops 1006632960 | bytes 786432 | tf_op jit(solution)/shard_map/grads/pallas_call | solution.py:270
  23.8 1.7 %grads.10 = (bf16[1,64,8,128]{3,2,1,0:T(8,128)(2,1)S(1)}, f32[3,2,256,128]{3,2,1,0:T(8,128)S(1)}) custom-call(bf16[1,2,64,8,128]{4,3,2,1,0:T(8,128)(2,1)S(1)} %collective-permute-done.10.refs_0_, bf16[2,256,128]{2,1,0:T(8,128)(2,1)S(1)} %collective-permute-done.3.refs_2_.refs_1_, bf16[2,256,128]{2,1,0:T(8,128)(2,1)S(1)} %collective-permute-done.4.refs_3_.refs_2_, ...), custom_call_target="tpu_custom_call" | custom-call | flops 503316480 | bytes 393216 | tf_op jit(solution)/shard_map/grads/pallas_call | solution.py:270
  25.5 0.0 collective-permute-done.12.refs_0_
  25.5 1.7 %grads.11 = (bf16[1,64,8,128]{3,2,1,0:T(8,128)(2,1)S(1)}, bf16[2,256,128]{2,1,0:T(8,128)(2,1)S(1)}, bf16[2,256,128]{2,1,0:T(8,128)(2,1)S(1)}, f32[2,256,128]{2,1,0:T(8,128)S(1)}) custom-call(bf16[1,2,64,8,128]{4,3,2,1,0:T(8,128)(2,1)S(1)} %collective-permute-done.12.refs_0_, bf16[2,256,128]{2,1,0:T(8,128)(2,1)S(1)} %collective-permute-done.3.refs_2_.refs_1_, ...), custom_call_target="tpu_custom_call" | custom-call | flops 503316480 | bytes 393216 | tf_op jit(solution)/shard_map/grads/pallas_call | solution.py:270
  27.1 1.6 %collective-permute-start.13 = (bf16[1,64,8,128]{3,2,1,0:T(8,128)(2,1)S(1)}, bf16[1,64,8,128]{3,2,1,0:T(8,128)(2,1)S(1)}, u32[]{:S(2)}, u32[]{:S(2)}) collective-permute-start(bf16[1,64,8,128]{3,2,1,0:T(8,128)(2,1)S(1)} %get-tuple-element.51), channel_id=1, source_target_pairs={{0,3},{1,2},{2,1},{3,0},{4,7},{5,6},{6,5},{7,4},{8,11},{9,10},{10,... | collective-permute-start | bytes 393224 | tf_op jit(solution)/shard_map/ppermute | solution.py:28
  28.7 0.9 %collective-permute-done.1.refs_2_.refs_1_ = bf16[2,256,128]{2,1,0:T(8,128)(2,1)S(1)} collective-permute-done((bf16[2,256,128]{2,1,0:T(8,128)(2,1)S(1)}, bf16[2,256,128]{2,1,0:T(8,128)(2,1)S(1)}, u32[]{:S(2)}, u32[]{:S(2)}) %collective-permute-start.1) | collective-permute-done | bytes 131104 | tf_op jit(solution)/shard_map/ppermute | solution.py:23
  29.7 2.5 %collective-permute-start.16 = (bf16[2,256,128]{2,1,0:T(8,128)(2,1)S(1)}, bf16[2,256,128]{2,1,0:T(8,128)(2,1)S(1)}, u32[]{:S(2)}, u32[]{:S(2)}) collective-permute-start(bf16[2,256,128]{2,1,0:T(8,128)(2,1)S(1)} %get-tuple-element.56), channel_id=1, source_target_pairs={{0,24},{4,28},{8,0},{12,4},{16,8},{20,12},{24,16},{28,20},{1,25},{... | collective-permute-start | bytes 393224 | tf_op jit(solution)/shard_map/ppermute | solution.py:23
  32.2 0.0 collective-permute-done.2.refs_3_.refs_2_
  32.2 2.8 %collective-permute-start.17 = (bf16[2,256,128]{2,1,0:T(8,128)(2,1)S(1)}, bf16[2,256,128]{2,1,0:T(8,128)(2,1)S(1)}, u32[]{:S(2)}, u32[]{:S(2)}) collective-permute-start(bf16[2,256,128]{2,1,0:T(8,128)(2,1)S(1)} %get-tuple-element.57), channel_id=1, source_target_pairs={{0,28},{4,0},{8,4},{12,8},{16,12},{20,16},{24,20},{28,24},{1,29},{... | collective-permute-start | bytes 393224 | tf_op jit(solution)/shard_map/ppermute | solution.py:23
  35.0 2.9 %grads.6 = (bf16[1,64,8,128]{3,2,1,0:T(8,128)(2,1)S(1)}, bf16[1,64,8,128]{3,2,1,0:T(8,128)(2,1)S(1)}, f32[3,2,256,128]{3,2,1,0:T(8,128)S(1)}) custom-call(bf16[2,2,64,8,128]{4,3,2,1,0:T(8,128)(2,1)S(1)} %get-tuple-element.32.refs_0_, bf16[2,2,64,8,128]{4,3,2,1,0:T(8,128)(2,1)S(1)} %collective-permute-done.refs_1_, ...), custom_call_target="tpu_custom_call" | custom-call | flops 1006632960 | bytes 786432 | tf_op jit(solution)/shard_map/grads/pallas_call | solution.py:270
  37.9 0.0 collective-permute-done.6.refs_0_
  37.9 1.7 %grads.8 = (bf16[1,64,8,128]{3,2,1,0:T(8,128)(2,1)S(1)}, f32[3,2,256,128]{3,2,1,0:T(8,128)S(1)}) custom-call(bf16[1,2,64,8,128]{4,3,2,1,0:T(8,128)(2,1)S(1)} %collective-permute-done.6.refs_0_, bf16[2,256,128]{2,1,0:T(8,128)(2,1)S(1)} %collective-permute-done.1.refs_2_.refs_1_, bf16[2,256,128]{2,1,0:T(8,128)(2,1)S(1)} %collective-permute-done.2.refs_3_.refs_2_, ...), custom_call_target="tpu_custom_call" | custom-call | flops 503316480 | bytes 393216 | tf_op jit(solution)/shard_map/grads/pallas_call | solution.py:270
  39.6 0.0 collective-permute-done.8.refs_0_
  39.6 1.7 %grads.9 = (bf16[1,64,8,128]{3,2,1,0:T(8,128)(2,1)S(1)}, bf16[2,256,128]{2,1,0:T(8,128)(2,1)S(1)}, bf16[2,256,128]{2,1,0:T(8,128)(2,1)S(1)}, f32[2,256,128]{2,1,0:T(8,128)S(1)}) custom-call(bf16[1,2,64,8,128]{4,3,2,1,0:T(8,128)(2,1)S(1)} %collective-permute-done.8.refs_0_, bf16[2,256,128]{2,1,0:T(8,128)(2,1)S(1)} %collective-permute-done.1.refs_2_.refs_1_, ...), custom_call_target="tpu_custom_call" | custom-call | flops 503316480 | bytes 393216 | tf_op jit(solution)/shard_map/grads/pallas_call | solution.py:270
  41.3 1.0 %collective-permute-start.14 = (bf16[2,256,128]{2,1,0:T(8,128)(2,1)S(1)}, bf16[2,256,128]{2,1,0:T(8,128)(2,1)S(1)}, u32[]{:S(2)}, u32[]{:S(2)}) collective-permute-start(bf16[2,256,128]{2,1,0:T(8,128)(2,1)S(1)} %get-tuple-element.53), channel_id=1, source_target_pairs={{0,24},{4,28},{8,0},{12,4},{16,8},{20,12},{24,16},{28,20},{1,25},{... | collective-permute-start | bytes 393224 | tf_op jit(solution)/shard_map/ppermute | solution.py:23
  42.4 0.1 collective-permute-start.5
  42.4 0.0 collective-permute-done.13.refs_6_
  42.4 1.6 %collective-permute-start.15 = (bf16[2,256,128]{2,1,0:T(8,128)(2,1)S(1)}, bf16[2,256,128]{2,1,0:T(8,128)(2,1)S(1)}, u32[]{:S(2)}, u32[]{:S(2)}) collective-permute-start(bf16[2,256,128]{2,1,0:T(8,128)(2,1)S(1)} %get-tuple-element.54), channel_id=1, source_target_pairs={{0,28},{4,0},{8,4},{12,8},{16,12},{20,16},{24,20},{28,24},{1,29},{... | collective-permute-start | bytes 393224 | tf_op jit(solution)/shard_map/ppermute | solution.py:23
  44.0 0.0 collective-permute-done.16.refs_11_
  44.0 1.2 %collective-permute-start.9 = (bf16[1,64,8,128]{3,2,1,0:T(8,128)(2,1)S(1)}, bf16[1,64,8,128]{3,2,1,0:T(8,128)(2,1)S(1)}, u32[]{:S(2)}, u32[]{:S(2)}) collective-permute-start(bf16[1,64,8,128]{3,2,1,0:T(8,128)(2,1)S(1)} %get-tuple-element.45), channel_id=1, source_target_pairs={{0,3},{1,2},{2,1},{3,0},{4,7},{5,6},{6,5},{7,4},{8,11},{9,10},{10,... | collective-permute-start | bytes 393224 | tf_op jit(solution)/shard_map/ppermute | solution.py:28
  45.3 0.0 collective-permute-done.17.refs_12_
  45.3 0.6 collective-permute-start.11
  45.8 2.9 %collective-permute-done.14.refs_8_ = bf16[2,256,128]{2,1,0:T(8,128)(2,1)S(1)} collective-permute-done((bf16[2,256,128]{2,1,0:T(8,128)(2,1)S(1)}, bf16[2,256,128]{2,1,0:T(8,128)(2,1)S(1)}, u32[]{:S(2)}, u32[]{:S(2)}) %collective-permute-start.14) | collective-permute-done | bytes 131104 | tf_op jit(solution)/shard_map/ppermute | solution.py:23
  48.7 1.6 %collective-permute-start.7 = (bf16[1,64,8,128]{3,2,1,0:T(8,128)(2,1)S(1)}, bf16[1,64,8,128]{3,2,1,0:T(8,128)(2,1)S(1)}, u32[]{:S(2)}, u32[]{:S(2)}) collective-permute-start(bf16[1,64,8,128]{3,2,1,0:T(8,128)(2,1)S(1)} %get-tuple-element.42), channel_id=1, source_target_pairs={{0,2},{1,3},{2,0},{3,1},{4,6},{5,7},{6,4},{7,5},{8,10},{9,11},{10,... | collective-permute-start | bytes 393224 | tf_op jit(solution)/shard_map/ppermute | solution.py:28
  50.3 0.7 %collective-permute-done.15.refs_9_ = bf16[2,256,128]{2,1,0:T(8,128)(2,1)S(1)} collective-permute-done((bf16[2,256,128]{2,1,0:T(8,128)(2,1)S(1)}, bf16[2,256,128]{2,1,0:T(8,128)(2,1)S(1)}, u32[]{:S(2)}, u32[]{:S(2)}) %collective-permute-start.15) | collective-permute-done | bytes 131104 | tf_op jit(solution)/shard_map/ppermute | solution.py:23
  51.0 0.0 collective-permute-done.9.refs_4_
  51.0 2.0 %collective-permute-done.11.refs_5_ = bf16[1,64,8,128]{3,2,1,0:T(8,128)(2,1)S(1)} collective-permute-done((bf16[1,64,8,128]{3,2,1,0:T(8,128)(2,1)S(1)}, bf16[1,64,8,128]{3,2,1,0:T(8,128)(2,1)S(1)}, u32[]{:S(2)}, u32[]{:S(2)}) %collective-permute-start.11) | collective-permute-done | bytes 131104 | tf_op jit(solution)/shard_map/ppermute | solution.py:28
  53.0 2.5 %collective-permute-done.7.refs_3_ = bf16[1,64,8,128]{3,2,1,0:T(8,128)(2,1)S(1)} collective-permute-done((bf16[1,64,8,128]{3,2,1,0:T(8,128)(2,1)S(1)}, bf16[1,64,8,128]{3,2,1,0:T(8,128)(2,1)S(1)}, u32[]{:S(2)}, u32[]{:S(2)}) %collective-permute-start.7) | collective-permute-done | bytes 131104 | tf_op jit(solution)/shard_map/ppermute | solution.py:28
  55.5 0.0 collective-permute-done.5.refs_2_
  55.5 1.1 %finish.1 = (bf16[64,8,8,128]{3,2,1,0:T(8,128)(2,1)}, bf16[512,128]{1,0:T(8,128)(2,1)}, bf16[512,128]{1,0:T(8,128)(2,1)}) custom-call(bf16[1,64,8,128]{3,2,1,0:T(8,128)(2,1)S(1)} %get-tuple-element.35.refs_0_, bf16[1,64,8,128]{3,2,1,0:T(8,128)(2,1)S(1)} %get-tuple-element.37.refs_1_, bf16[2,64,8,128]{3,2,1,0:T(8,128)(2,1)S(1)} %collective-permute-done.5.refs_2_, ...), custom_call_target="tpu_custom_call" | custom-call | tf_op jit(solution)/shard_map/finish/pallas_call | solution.py:149
  (1 shorter events, 0.0 us)
Async XLA Ops:
  2.2 18.4 %collective-permute-start = (bf16[2,2,64,8,128]{4,3,2,1,0:T(8,128)(2,1)S(1)}, bf16[2,2,64,8,128]{4,3,2,1,0:T(8,128)(2,1)S(1)}, u32[]{:S(2)}, u32[]{:S(2)}) collective-permute-start(bf16[2,2,64,8,128]{4,3,2,1,0:T(8,128)(2,1)S(1)} %get-tuple-element.33), channel_id=1, source_target_pairs={{0,1},{1,0},{2,3},{3,2},{4,5},{5,4},{6,7},{7,6},{8,9},{9,8},{10,11... | collective-permute-start | bytes 1572872 | tf_op jit(solution)/shard_map/ppermute | solution.py:28
  2.8 17.3 %collective-permute-start.10 = (bf16[1,2,64,8,128]{4,3,2,1,0:T(8,128)(2,1)S(1)}, bf16[1,2,64,8,128]{4,3,2,1,0:T(8,128)(2,1)S(1)}, u32[]{:S(2)}, u32[]{:S(2)}) collective-permute-start(bf16[1,2,64,8,128]{4,3,2,1,0:T(8,128)(2,1)S(1)} %get-tuple-element.46), channel_id=1, source_target_pairs={{0,2},{1,3},{2,0},{3,1},{4,6},{5,7},{6,4},{7,5},{8,10},{9,11},{10,... | collective-permute-start | bytes 786440 | tf_op jit(solution)/shard_map/ppermute | solution.py:28
  6.6 13.0 %collective-permute-start.3 = (bf16[2,256,128]{2,1,0:T(8,128)(2,1)S(1)}, bf16[2,256,128]{2,1,0:T(8,128)(2,1)S(1)}, u32[]{:S(2)}, u32[]{:S(2)}) collective-permute-start(bf16[2,256,128]{2,1,0:T(8,128)(2,1)S(1)} %get-tuple-element.36.refs_4_.refs_3_), channel_id=1, source_target_pairs={{0,8},{4,12},{8,16},{12,20},{16,24},{20,28},{24,0},{28,4},{1,9},{5... | collective-permute-start | bytes 393224 | tf_op jit(solution)/shard_map/ppermute | solution.py:23
  9.3 10.4 %collective-permute-start.4 = (bf16[2,256,128]{2,1,0:T(8,128)(2,1)S(1)}, bf16[2,256,128]{2,1,0:T(8,128)(2,1)S(1)}, u32[]{:S(2)}, u32[]{:S(2)}) collective-permute-start(bf16[2,256,128]{2,1,0:T(8,128)(2,1)S(1)} %get-tuple-element.36.refs_4_.refs_3_), channel_id=1, source_target_pairs={{0,4},{4,8},{8,12},{12,16},{16,20},{20,24},{24,28},{28,0},{1,5},{5... | collective-permute-start | bytes 393224 | tf_op jit(solution)/shard_map/ppermute | solution.py:23
  10.8 14.6 %collective-permute-start.12 = (bf16[1,2,64,8,128]{4,3,2,1,0:T(8,128)(2,1)S(1)}, bf16[1,2,64,8,128]{4,3,2,1,0:T(8,128)(2,1)S(1)}, u32[]{:S(2)}, u32[]{:S(2)}) collective-permute-start(bf16[1,2,64,8,128]{4,3,2,1,0:T(8,128)(2,1)S(1)} %get-tuple-element.49), channel_id=1, source_target_pairs={{0,3},{1,2},{2,1},{3,0},{4,7},{5,6},{6,5},{7,4},{8,11},{9,10},{10,... | collective-permute-start | bytes 786440 | tf_op jit(solution)/shard_map/ppermute | solution.py:28
  19.6 10.0 %collective-permute-start.1 = (bf16[2,256,128]{2,1,0:T(8,128)(2,1)S(1)}, bf16[2,256,128]{2,1,0:T(8,128)(2,1)S(1)}, u32[]{:S(2)}, u32[]{:S(2)}) collective-permute-start(bf16[2,256,128]{2,1,0:T(8,128)(2,1)S(1)} %get-tuple-element.34.refs_4_.refs_3_), channel_id=1, source_target_pairs={{0,8},{4,12},{8,16},{12,20},{16,24},{20,28},{24,0},{28,4},{1,9},{5... | collective-permute-start | bytes 393224 | tf_op jit(solution)/shard_map/ppermute | solution.py:23
  19.7 12.5 %collective-permute-start.2 = (bf16[2,256,128]{2,1,0:T(8,128)(2,1)S(1)}, bf16[2,256,128]{2,1,0:T(8,128)(2,1)S(1)}, u32[]{:S(2)}, u32[]{:S(2)}) collective-permute-start(bf16[2,256,128]{2,1,0:T(8,128)(2,1)S(1)} %get-tuple-element.34.refs_4_.refs_3_), channel_id=1, source_target_pairs={{0,4},{4,8},{8,12},{12,16},{16,20},{20,24},{24,28},{28,0},{1,5},{5... | collective-permute-start | bytes 393224 | tf_op jit(solution)/shard_map/ppermute | solution.py:23
  20.1 17.8 %collective-permute-start.6 = (bf16[1,2,64,8,128]{4,3,2,1,0:T(8,128)(2,1)S(1)}, bf16[1,2,64,8,128]{4,3,2,1,0:T(8,128)(2,1)S(1)}, u32[]{:S(2)}, u32[]{:S(2)}) collective-permute-start(bf16[1,2,64,8,128]{4,3,2,1,0:T(8,128)(2,1)S(1)} %get-tuple-element.40), channel_id=1, source_target_pairs={{0,2},{1,3},{2,0},{3,1},{4,6},{5,7},{6,4},{7,5},{8,10},{9,11},{10,... | collective-permute-start | bytes 786440 | tf_op jit(solution)/shard_map/ppermute | solution.py:28
  20.6 19.0 %collective-permute-start.8 = (bf16[1,2,64,8,128]{4,3,2,1,0:T(8,128)(2,1)S(1)}, bf16[1,2,64,8,128]{4,3,2,1,0:T(8,128)(2,1)S(1)}, u32[]{:S(2)}, u32[]{:S(2)}) collective-permute-start(bf16[1,2,64,8,128]{4,3,2,1,0:T(8,128)(2,1)S(1)} %get-tuple-element.43), channel_id=1, source_target_pairs={{0,3},{1,2},{2,1},{3,0},{4,7},{5,6},{6,5},{7,4},{8,11},{9,10},{10,... | collective-permute-start | bytes 786440 | tf_op jit(solution)/shard_map/ppermute | solution.py:28
  27.1 15.3 %collective-permute-start.13 = (bf16[1,64,8,128]{3,2,1,0:T(8,128)(2,1)S(1)}, bf16[1,64,8,128]{3,2,1,0:T(8,128)(2,1)S(1)}, u32[]{:S(2)}, u32[]{:S(2)}) collective-permute-start(bf16[1,64,8,128]{3,2,1,0:T(8,128)(2,1)S(1)} %get-tuple-element.51), channel_id=1, source_target_pairs={{0,3},{1,2},{2,1},{3,0},{4,7},{5,6},{6,5},{7,4},{8,11},{9,10},{10,... | collective-permute-start | bytes 393224 | tf_op jit(solution)/shard_map/ppermute | solution.py:28
  29.7 14.3 %collective-permute-start.16 = (bf16[2,256,128]{2,1,0:T(8,128)(2,1)S(1)}, bf16[2,256,128]{2,1,0:T(8,128)(2,1)S(1)}, u32[]{:S(2)}, u32[]{:S(2)}) collective-permute-start(bf16[2,256,128]{2,1,0:T(8,128)(2,1)S(1)} %get-tuple-element.56), channel_id=1, source_target_pairs={{0,24},{4,28},{8,0},{12,4},{16,8},{20,12},{24,16},{28,20},{1,25},{... | collective-permute-start | bytes 393224 | tf_op jit(solution)/shard_map/ppermute | solution.py:23
  32.2 13.1 %collective-permute-start.17 = (bf16[2,256,128]{2,1,0:T(8,128)(2,1)S(1)}, bf16[2,256,128]{2,1,0:T(8,128)(2,1)S(1)}, u32[]{:S(2)}, u32[]{:S(2)}) collective-permute-start(bf16[2,256,128]{2,1,0:T(8,128)(2,1)S(1)} %get-tuple-element.57), channel_id=1, source_target_pairs={{0,28},{4,0},{8,4},{12,8},{16,12},{20,16},{24,20},{28,24},{1,29},{... | collective-permute-start | bytes 393224 | tf_op jit(solution)/shard_map/ppermute | solution.py:23
  41.3 7.4 %collective-permute-start.14 = (bf16[2,256,128]{2,1,0:T(8,128)(2,1)S(1)}, bf16[2,256,128]{2,1,0:T(8,128)(2,1)S(1)}, u32[]{:S(2)}, u32[]{:S(2)}) collective-permute-start(bf16[2,256,128]{2,1,0:T(8,128)(2,1)S(1)} %get-tuple-element.53), channel_id=1, source_target_pairs={{0,24},{4,28},{8,0},{12,4},{16,8},{20,12},{24,16},{28,20},{1,25},{... | collective-permute-start | bytes 393224 | tf_op jit(solution)/shard_map/ppermute | solution.py:23
  42.4 13.1 %collective-permute-start.5 = (bf16[2,64,8,128]{3,2,1,0:T(8,128)(2,1)S(1)}, bf16[2,64,8,128]{3,2,1,0:T(8,128)(2,1)S(1)}, u32[]{:S(2)}, u32[]{:S(2)}) collective-permute-start(bf16[2,64,8,128]{3,2,1,0:T(8,128)(2,1)S(1)} %pad_maximum_fusion), channel_id=1, source_target_pairs={{0,1},{1,0},{2,3},{3,2},{4,5},{5,4},{6,7},{7,6},{8,9},{9,8},{10,11... | collective-permute-start | bytes 786440 | tf_op jit(solution)/shard_map/ppermute | solution.py:28
  42.4 8.5 %collective-permute-start.15 = (bf16[2,256,128]{2,1,0:T(8,128)(2,1)S(1)}, bf16[2,256,128]{2,1,0:T(8,128)(2,1)S(1)}, u32[]{:S(2)}, u32[]{:S(2)}) collective-permute-start(bf16[2,256,128]{2,1,0:T(8,128)(2,1)S(1)} %get-tuple-element.54), channel_id=1, source_target_pairs={{0,28},{4,0},{8,4},{12,8},{16,12},{20,16},{24,20},{28,24},{1,29},{... | collective-permute-start | bytes 393224 | tf_op jit(solution)/shard_map/ppermute | solution.py:23
  44.0 6.9 %collective-permute-start.9 = (bf16[1,64,8,128]{3,2,1,0:T(8,128)(2,1)S(1)}, bf16[1,64,8,128]{3,2,1,0:T(8,128)(2,1)S(1)}, u32[]{:S(2)}, u32[]{:S(2)}) collective-permute-start(bf16[1,64,8,128]{3,2,1,0:T(8,128)(2,1)S(1)} %get-tuple-element.45), channel_id=1, source_target_pairs={{0,3},{1,2},{2,1},{3,0},{4,7},{5,6},{6,5},{7,4},{8,11},{9,10},{10,... | collective-permute-start | bytes 393224 | tf_op jit(solution)/shard_map/ppermute | solution.py:28
  45.3 7.7 %collective-permute-start.11 = (bf16[1,64,8,128]{3,2,1,0:T(8,128)(2,1)S(1)}, bf16[1,64,8,128]{3,2,1,0:T(8,128)(2,1)S(1)}, u32[]{:S(2)}, u32[]{:S(2)}) collective-permute-start(bf16[1,64,8,128]{3,2,1,0:T(8,128)(2,1)S(1)} %get-tuple-element.48), channel_id=1, source_target_pairs={{0,2},{1,3},{2,0},{3,1},{4,6},{5,7},{6,4},{7,5},{8,10},{9,11},{10,... | collective-permute-start | bytes 393224 | tf_op jit(solution)/shard_map/ppermute | solution.py:28
  48.7 6.8 %collective-permute-start.7 = (bf16[1,64,8,128]{3,2,1,0:T(8,128)(2,1)S(1)}, bf16[1,64,8,128]{3,2,1,0:T(8,128)(2,1)S(1)}, u32[]{:S(2)}, u32[]{:S(2)}) collective-permute-start(bf16[1,64,8,128]{3,2,1,0:T(8,128)(2,1)S(1)} %get-tuple-element.42), channel_id=1, source_target_pairs={{0,2},{1,3},{2,0},{3,1},{4,6},{5,7},{6,4},{7,5},{8,10},{9,11},{10,... | collective-permute-start | bytes 393224 | tf_op jit(solution)/shard_map/ppermute | solution.py:28
where the time goes:
time: 56.9 us; the launch traced here: 56.8 us
  starting transfers between devices  21.5 us (38%)
  waiting for transfers between devices  17.8 us (31%)
  Pallas kernels  16.5 us (29%)
  between operations  0.88 us (2%)
    ppermute x8, waiting for transfers between devices, shifted(): return lax.ppermute(value, SEQ, pairs)  13.3 us
    ppermute x8, starting transfers between devices, shifted(): return lax.ppermute(value, SEQ, pairs)  12.6 us
    pallas_call x6, Pallas kernels, group_grads(): pl.pallas_call(functools.partial(grads_kernel, where, distances, sums is...  12.5 us
    ppermute x10, starting transfers between devices, swapped(): lax.ppermute(value, 'head', [(i, i ^ distance) for i in range(peers)])  8.89 us
    ppermute x10, waiting for transfers between devices, swapped(): lax.ppermute(value, 'head', [(i, i ^ distance) for i in range(peers)])  4.5 us
    pallas_call x1, Pallas kernels, pack(): pl.pallas_call(functools.partial(pack_kernel, parts, kv_heads), in_specs=...  1.6 us
    pallas_call x1, Pallas kernels, pack_first(): pl.pallas_call(functools.partial(first_kernel, parts, kv_heads), in_specs...  1.27 us
  transfers between devices with their start and end apart: 18, of which 6 were waited for; matrix products, arithmetic and copies ran while one was open for 0% of the time, Pallas kernels for 24%

commit v1 on v0

--- a/solution.py
+++ b/solution.py
@@ -115,17 +115,43 @@
     return outs[:kv_heads], outs[kv_heads:]
 
 
-def finish_kernel(parts, heads, *refs):
-    values, totals = refs[: len(parts)], refs[len(parts) : len(parts) + 3 * heads]
-    dq_ref, dk_ref, dv_ref, wide, narrow, sem = refs[len(parts) + 3 * heads :]
+def place_copies(values, parts, out_ref, sem, heads):
     me = lax.axis_index("head")
     copies = []
     for value, part in zip(values, parts):
         for n, (kv, distance) in enumerate(part):
             place = (me ^ distance) * heads + kv
             copies.append(
-                pltpu.make_async_copy(value.at[n], dq_ref.at[:, place], sem.at[len(copies)])
+                pltpu.make_async_copy(value.at[n], out_ref.at[:, place], sem.at[len(copies)])
             )
+    return copies
+
+
+def store_kernel(parts, heads, *refs):
+    copies = place_copies(refs[:-2], parts, refs[-2], refs[-1], heads)
+    for copy in copies:
+        copy.start()
+    for copy in copies:
+        copy.wait()
+
+
+def store(values, parts, places, heads):
+    _, part_rows, group, width = values[0].shape
+    return pl.pallas_call(
+        functools.partial(store_kernel, parts, heads),
+        in_specs=[VMEM] * len(values),
+        out_specs=HBM,
+        out_shape=pltpu.HBM((part_rows, places, group, width), jnp.bfloat16),
+        scratch_shapes=[pltpu.SemaphoreType.DMA((sum(len(part) for part in parts),))],
+        compiler_params=pltpu.CompilerParams(vmem_limit_bytes=16 * 2**20),
+        name="store",
+    )(*values)
+
+
+def finish_kernel(parts, heads, old_ref, *refs):
+    values, totals = refs[: len(parts)], refs[len(parts) : len(parts) + 3 * heads]
+    dq_ref, dk_ref, dv_ref, wide, narrow, sem = refs[len(parts) + 3 * heads :]
+    copies = place_copies(values, parts, dq_ref, sem, heads)
     for copy in copies:
         copy.start()
     tok_rows = totals[0].shape[1]
@@ -141,28 +167,28 @@
         copy.wait()
 
 
-def finish(values, parts, totals):
-    _, part_rows, group, width = values[0].shape
+def finish(stored, values, parts, totals):
+    part_rows, places, group, width = stored.shape
     heads = len(totals)
     tok_rows = totals[0][0].shape[1]
-    places = sum(len(part) for part in parts)
     dq, dk, dv = pl.pallas_call(
         functools.partial(finish_kernel, parts, heads),
-        in_specs=[VMEM] * (len(values) + 3 * heads),
+        in_specs=[HBM] + [VMEM] * (len(values) + 3 * heads),
         out_specs=[HBM] * 3,
         out_shape=[
-            jax.ShapeDtypeStruct((part_rows, places, group, width), jnp.bfloat16),
-            jax.ShapeDtypeStruct((tok_rows * heads, width), jnp.bfloat16),
-            jax.ShapeDtypeStruct((tok_rows * heads, width), jnp.bfloat16),
+            pltpu.HBM((part_rows, places, group, width), jnp.bfloat16),
+            pltpu.HBM((tok_rows * heads, width), jnp.bfloat16),
+            pltpu.HBM((tok_rows * heads, width), jnp.bfloat16),
         ],
         scratch_shapes=[
             pltpu.VMEM((2, tok_rows * heads, width), jnp.float32),
             pltpu.VMEM((2, tok_rows * heads, width), jnp.bfloat16),
-            pltpu.SemaphoreType.DMA((places + 2,)),
-        ],
+            pltpu.SemaphoreType.DMA((sum(len(part) for part in parts) + 2,)),
+        ],
+        input_output_aliases={0: 0},
         compiler_params=pltpu.CompilerParams(vmem_limit_bytes=16 * 2**20),
         name="finish",
-    )(*values, *(term for total in totals for term in total))
+    )(stored, *values, *(term for total in totals for term in total))
     return (
         dq.reshape(part_rows, places * group, width),
         dk.reshape(tok_rows, heads, width),
@@ -341,10 +367,12 @@
         dnear = shifted(sums[1], -1)
         totals.append((sums[2], dfar, dnear))
     dq_partner = swapped(jnp.concatenate([dq[kv, 1] for kv in all_kv], axis=0), 1)
-    parts = [[(kv, 0)] for kv in all_kv] + [[(kv, 1) for kv in all_kv]]
-    parts += [[(kv, d)] for kv in all_kv for d in far_cores]
-    values = [dq[part[0]] if len(part) == 1 else dq_partner for part in parts]
-    return finish(values, parts, totals)
+    early = [[(kv, 0)] for kv in all_kv] + [[(kv, 1) for kv in all_kv]]
+    early += [[(kv, d)] for kv in all_kv[:-1] for d in far_cores]
+    values = [dq[part[0]] if len(part) == 1 else dq_partner for part in early]
+    stored = store(values, early, places, kv_heads)
+    late = [(all_kv[-1], d) for d in far_cores]
+    return finish(stored, [dq[key] for key in late], [[key] for key in late], totals)
 
 
 def solution(mesh):

time: 56.9 us -> 70.2 us (1.23)
  waiting for transfers between devices: 17.8 us -> 32 us
  starting transfers between devices: 21.5 us -> 20.1 us
    ppermute x10, waiting for transfers between devices: 4.5 us -> 13.2 us  [swapped(): lax.ppermute(value, 'head', [(i, i ^ distance) for i in range(peers)])]
    ppermute x8, waiting for transfers between devices: 13.3 us -> 18.8 us  [shifted(): return lax.ppermute(value, SEQ, pairs)]
    ppermute x8, starting transfers between devices: 12.6 us -> 9.59 us  [shifted(): return lax.ppermute(value, SEQ, pairs)]
    ppermute x10, starting transfers between devices: 8.89 us -> 10.5 us  [swapped(): lax.ppermute(value, 'head', [(i, i ^ distance) for i in range(peers)])]
    pallas_call x0 -> x1, Pallas kernels: none -> 0.92 us  [store(): pl.pallas_call(functools.partial(store_kernel, parts, heads), in_specs=[V...]
  transfers between devices with their start and end apart: 18 -> 18, of which waited for: 6 -> 8; matrix products, arithmetic and copies ran while one was open for 0% -> 0% of each run, Pallas kernels for 24% -> 21%
where the time goes in v1:
time: 70.2 us; the launch traced here: 70 us
  waiting for transfers between devices  32 us (46%)
  starting transfers between devices  20.1 us (29%)
  Pallas kernels  17.1 us (24%)
  between operations  0.71 us (1%)
    ppermute x8, waiting for transfers between devices, shifted(): return lax.ppermute(value, SEQ, pairs)  18.8 us
    ppermute x10, waiting for transfers between devices, swapped(): lax.ppermute(value, 'head', [(i, i ^ distance) for i in range(peers)])  13.2 us
    pallas_call x6, Pallas kernels, group_grads(): pl.pallas_call(functools.partial(grads_kernel, where, distances, sums is...  12.5 us
    ppermute x10, starting transfers between devices, swapped(): lax.ppermute(value, 'head', [(i, i ^ distance) for i in range(peers)])  10.5 us
    ppermute x8, starting transfers between devices, shifted(): return lax.ppermute(value, SEQ, pairs)  9.59 us
    pallas_call x1, Pallas kernels, pack(): pl.pallas_call(functools.partial(pack_kernel, parts, kv_heads), in_specs=...  1.6 us
  transfers between devices with their start and end apart: 18, of which 8 were waited for; matrix products, arithmetic and copies ran while one was open for 0% of the time, Pallas kernels for 21%

profile of v1, /device:TPU:0, one launch (start us, length us, event | category | flops | bytes accessed | tf_op | source)
XLA Modules:
  0.0 70.0 jit_solution(5026500209083946661)
XLA Ops:
  0.6 1.6 %pack.1 = (bf16[2,2,64,8,128]{4,3,2,1,0:T(8,128)(2,1)S(1)}, bf16[2,2,64,8,128]{4,3,2,1,0:T(8,128)(2,1)S(1)}, bf16[1,2,64,8,128]{4,3,2,1,0:T(8,128)(2,1)S(1)}, bf16[1,2,64,8,128]{4,3,2,1,0:T(8,128)(2,1)S(1)}) custom-call(bf16[64,8,8,128]{3,2,1,0:T(8,128)(2,1)} %bitcast.8, bf16[64,8,8,128]{3,2,1,0:T(8,128)(2,1)} %bitcast.10), custom_call_target="tpu_custom_call" | custom-call | tf_op jit(solution)/shard_map/pack/pallas_call | solution.py:79
  2.2 0.6 collective-permute-start
  2.8 1.3 %first.1 = (bf16[2,256,128]{2,1,0:T(8,128)(2,1)S(1)}, bf16[2,256,128]{2,1,0:T(8,128)(2,1)S(1)}, bf16[1,2,64,8,128]{4,3,2,1,0:T(8,128)(2,1)S(1)}, bf16[1,2,64,8,128]{4,3,2,1,0:T(8,128)(2,1)S(1)}) custom-call(bf16[512,128]{1,0:T(8,128)(2,1)} %bitcast.12, bf16[512,128]{1,0:T(8,128)(2,1)} %bitcast.13, bf16[64,8,8,128]{3,2,1,0:T(8,128)(2,1)} %bitcast.9, ...), custom_call_target="tpu_custom_call" | custom-call | tf_op jit(solution)/shard_map/first/pallas_call | solution.py:95
  4.1 3.6 %collective-permute-start.3 = (bf16[2,256,128]{2,1,0:T(8,128)(2,1)S(1)}, bf16[2,256,128]{2,1,0:T(8,128)(2,1)S(1)}, u32[]{:S(2)}, u32[]{:S(2)}) collective-permute-start(bf16[2,256,128]{2,1,0:T(8,128)(2,1)S(1)} %get-tuple-element.36.refs_4_.refs_3_), channel_id=1, source_target_pairs={{0,8},{4,12},{8,16},{12,20},{16,24},{20,28},{24,0},{28,4},{1,9},{5... | collective-permute-start | bytes 393224 | tf_op jit(solution)/shard_map/ppermute | solution.py:23
  7.7 1.6 %collective-permute-start.4 = (bf16[2,256,128]{2,1,0:T(8,128)(2,1)S(1)}, bf16[2,256,128]{2,1,0:T(8,128)(2,1)S(1)}, u32[]{:S(2)}, u32[]{:S(2)}) collective-permute-start(bf16[2,256,128]{2,1,0:T(8,128)(2,1)S(1)} %get-tuple-element.36.refs_4_.refs_3_), channel_id=1, source_target_pairs={{0,4},{4,8},{8,12},{12,16},{16,20},{20,24},{24,28},{28,0},{1,5},{5... | collective-permute-start | bytes 393224 | tf_op jit(solution)/shard_map/ppermute | solution.py:23
  9.3 1.3 %collective-permute-start.1 = (bf16[2,256,128]{2,1,0:T(8,128)(2,1)S(1)}, bf16[2,256,128]{2,1,0:T(8,128)(2,1)S(1)}, u32[]{:S(2)}, u32[]{:S(2)}) collective-permute-start(bf16[2,256,128]{2,1,0:T(8,128)(2,1)S(1)} %get-tuple-element.34.refs_4_.refs_3_), channel_id=1, source_target_pairs={{0,8},{4,12},{8,16},{12,20},{16,24},{20,28},{24,0},{28,4},{1,9},{5... | collective-permute-start | bytes 393224 | tf_op jit(solution)/shard_map/ppermute | solution.py:23
  10.6 2.5 %collective-permute-start.2 = (bf16[2,256,128]{2,1,0:T(8,128)(2,1)S(1)}, bf16[2,256,128]{2,1,0:T(8,128)(2,1)S(1)}, u32[]{:S(2)}, u32[]{:S(2)}) collective-permute-start(bf16[2,256,128]{2,1,0:T(8,128)(2,1)S(1)} %get-tuple-element.34.refs_4_.refs_3_), channel_id=1, source_target_pairs={{0,4},{4,8},{8,12},{12,16},{16,20},{20,24},{24,28},{28,0},{1,5},{5... | collective-permute-start | bytes 393224 | tf_op jit(solution)/shard_map/ppermute | solution.py:23
  13.1 11.2 %collective-permute-done.3.refs_2_.refs_1_ = bf16[2,256,128]{2,1,0:T(8,128)(2,1)S(1)} collective-permute-done((bf16[2,256,128]{2,1,0:T(8,128)(2,1)S(1)}, bf16[2,256,128]{2,1,0:T(8,128)(2,1)S(1)}, u32[]{:S(2)}, u32[]{:S(2)}) %collective-permute-start.3) | collective-permute-done | bytes 131104 | tf_op jit(solution)/shard_map/ppermute | solution.py:23
  24.3 1.8 %collective-permute-start.10 = (bf16[1,2,64,8,128]{4,3,2,1,0:T(8,128)(2,1)S(1)}, bf16[1,2,64,8,128]{4,3,2,1,0:T(8,128)(2,1)S(1)}, u32[]{:S(2)}, u32[]{:S(2)}) collective-permute-start(bf16[1,2,64,8,128]{4,3,2,1,0:T(8,128)(2,1)S(1)} %get-tuple-element.46), channel_id=1, source_target_pairs={{0,2},{1,3},{2,0},{3,1},{4,6},{5,7},{6,4},{7,5},{8,10},{9,11},{10,... | collective-permute-start | bytes 786440 | tf_op jit(solution)/shard_map/ppermute | solution.py:28
  26.0 0.0 collective-permute-done.4.refs_3_.refs_2_
  26.0 0.0 collective-permute-start.12
  26.0 0.0 collective-permute-done.refs_1_
  26.0 0.5 collective-permute-start.6
  26.5 2.9 %grads.7 = (bf16[1,64,8,128]{3,2,1,0:T(8,128)(2,1)S(1)}, bf16[1,64,8,128]{3,2,1,0:T(8,128)(2,1)S(1)}, f32[3,2,256,128]{3,2,1,0:T(8,128)S(1)}) custom-call(bf16[2,2,64,8,128]{4,3,2,1,0:T(8,128)(2,1)S(1)} %get-tuple-element.32.refs_0_, bf16[2,2,64,8,128]{4,3,2,1,0:T(8,128)(2,1)S(1)} %collective-permute-done.refs_1_, ...), custom_call_target="tpu_custom_call" | custom-call | flops 1006632960 | bytes 786432 | tf_op jit(solution)/shard_map/grads/pallas_call | solution.py:296
  29.4 0.0 collective-permute-done.1.refs_2_.refs_1_
  29.4 1.3 %collective-permute-start.8 = (bf16[1,2,64,8,128]{4,3,2,1,0:T(8,128)(2,1)S(1)}, bf16[1,2,64,8,128]{4,3,2,1,0:T(8,128)(2,1)S(1)}, u32[]{:S(2)}, u32[]{:S(2)}) collective-permute-start(bf16[1,2,64,8,128]{4,3,2,1,0:T(8,128)(2,1)S(1)} %get-tuple-element.43), channel_id=1, source_target_pairs={{0,3},{1,2},{2,1},{3,0},{4,7},{5,6},{6,5},{7,4},{8,11},{9,10},{10,... | collective-permute-start | bytes 786440 | tf_op jit(solution)/shard_map/ppermute | solution.py:28
  30.7 0.0 collective-permute-done.2.refs_3_.refs_2_
  30.8 2.9 %grads.6 = (bf16[1,64,8,128]{3,2,1,0:T(8,128)(2,1)S(1)}, bf16[1,64,8,128]{3,2,1,0:T(8,128)(2,1)S(1)}, f32[3,2,256,128]{3,2,1,0:T(8,128)S(1)}) custom-call(bf16[2,2,64,8,128]{4,3,2,1,0:T(8,128)(2,1)S(1)} %get-tuple-element.32.refs_0_, bf16[2,2,64,8,128]{4,3,2,1,0:T(8,128)(2,1)S(1)} %collective-permute-done.refs_1_, ...), custom_call_target="tpu_custom_call" | custom-call | flops 1006632960 | bytes 786432 | tf_op jit(solution)/shard_map/grads/pallas_call | solution.py:296
  33.7 0.5 collective-permute-start.5
  34.2 0.0 collective-permute-done.10.refs_0_
  34.2 1.7 %grads.10 = (bf16[1,64,8,128]{3,2,1,0:T(8,128)(2,1)S(1)}, f32[3,2,256,128]{3,2,1,0:T(8,128)S(1)}) custom-call(bf16[1,2,64,8,128]{4,3,2,1,0:T(8,128)(2,1)S(1)} %collective-permute-done.10.refs_0_, bf16[2,256,128]{2,1,0:T(8,128)(2,1)S(1)} %collective-permute-done.3.refs_2_.refs_1_, bf16[2,256,128]{2,1,0:T(8,128)(2,1)S(1)} %collective-permute-done.4.refs_3_.refs_2_, ...), custom_call_target="tpu_custom_call" | custom-call | flops 503316480 | bytes 393216 | tf_op jit(solution)/shard_map/grads/pallas_call | solution.py:296
  35.9 2.4 %collective-permute-done.12.refs_0_ = bf16[1,2,64,8,128]{4,3,2,1,0:T(8,128)(2,1)S(1)} collective-permute-done((bf16[1,2,64,8,128]{4,3,2,1,0:T(8,128)(2,1)S(1)}, bf16[1,2,64,8,128]{4,3,2,1,0:T(8,128)(2,1)S(1)}, u32[]{:S(2)}, u32[]{:S(2)}) %collective-permute-start.12) | collective-permute-done | bytes 262176 | tf_op jit(solution)/shard_map/ppermute | solution.py:28
  38.3 1.7 %grads.11 = (bf16[1,64,8,128]{3,2,1,0:T(8,128)(2,1)S(1)}, bf16[2,256,128]{2,1,0:T(8,128)(2,1)S(1)}, bf16[2,256,128]{2,1,0:T(8,128)(2,1)S(1)}, f32[2,256,128]{2,1,0:T(8,128)S(1)}) custom-call(bf16[1,2,64,8,128]{4,3,2,1,0:T(8,128)(2,1)S(1)} %collective-permute-done.12.refs_0_, bf16[2,256,128]{2,1,0:T(8,128)(2,1)S(1)} %collective-permute-done.3.refs_2_.refs_1_, ...), custom_call_target="tpu_custom_call" | custom-call | flops 503316480 | bytes 393216 | tf_op jit(solution)/shard_map/grads/pallas_call | solution.py:296
  40.0 2.0 %collective-permute-start.13 = (bf16[1,64,8,128]{3,2,1,0:T(8,128)(2,1)S(1)}, bf16[1,64,8,128]{3,2,1,0:T(8,128)(2,1)S(1)}, u32[]{:S(2)}, u32[]{:S(2)}) collective-permute-start(bf16[1,64,8,128]{3,2,1,0:T(8,128)(2,1)S(1)} %get-tuple-element.51), channel_id=1, source_target_pairs={{0,3},{1,2},{2,1},{3,0},{4,7},{5,6},{6,5},{7,4},{8,11},{9,10},{10,... | collective-permute-start | bytes 393224 | tf_op jit(solution)/shard_map/ppermute | solution.py:28
  42.0 2.7 %collective-permute-done.6.refs_0_ = bf16[1,2,64,8,128]{4,3,2,1,0:T(8,128)(2,1)S(1)} collective-permute-done((bf16[1,2,64,8,128]{4,3,2,1,0:T(8,128)(2,1)S(1)}, bf16[1,2,64,8,128]{4,3,2,1,0:T(8,128)(2,1)S(1)}, u32[]{:S(2)}, u32[]{:S(2)}) %collective-permute-start.6) | collective-permute-done | bytes 262176 | tf_op jit(solution)/shard_map/ppermute | solution.py:28
  44.7 1.7 %grads.8 = (bf16[1,64,8,128]{3,2,1,0:T(8,128)(2,1)S(1)}, f32[3,2,256,128]{3,2,1,0:T(8,128)S(1)}) custom-call(bf16[1,2,64,8,128]{4,3,2,1,0:T(8,128)(2,1)S(1)} %collective-permute-done.6.refs_0_, bf16[2,256,128]{2,1,0:T(8,128)(2,1)S(1)} %collective-permute-done.1.refs_2_.refs_1_, bf16[2,256,128]{2,1,0:T(8,128)(2,1)S(1)} %collective-permute-done.2.refs_3_.refs_2_, ...), custom_call_target="tpu_custom_call" | custom-call | flops 503316480 | bytes 393216 | tf_op jit(solution)/shard_map/grads/pallas_call | solution.py:296
  46.4 2.8 %collective-permute-done.8.refs_0_ = bf16[1,2,64,8,128]{4,3,2,1,0:T(8,128)(2,1)S(1)} collective-permute-done((bf16[1,2,64,8,128]{4,3,2,1,0:T(8,128)(2,1)S(1)}, bf16[1,2,64,8,128]{4,3,2,1,0:T(8,128)(2,1)S(1)}, u32[]{:S(2)}, u32[]{:S(2)}) %collective-permute-start.8) | collective-permute-done | bytes 262176 | tf_op jit(solution)/shard_map/ppermute | solution.py:28
  49.2 1.7 %grads.9 = (bf16[1,64,8,128]{3,2,1,0:T(8,128)(2,1)S(1)}, bf16[2,256,128]{2,1,0:T(8,128)(2,1)S(1)}, bf16[2,256,128]{2,1,0:T(8,128)(2,1)S(1)}, f32[2,256,128]{2,1,0:T(8,128)S(1)}) custom-call(bf16[1,2,64,8,128]{4,3,2,1,0:T(8,128)(2,1)S(1)} %collective-permute-done.8.refs_0_, bf16[2,256,128]{2,1,0:T(8,128)(2,1)S(1)} %collective-permute-done.1.refs_2_.refs_1_, ...), custom_call_target="tpu_custom_call" | custom-call | flops 503316480 | bytes 393216 | tf_op jit(solution)/shard_map/grads/pallas_call | solution.py:296
  50.8 2.0 %collective-permute-start.9 = (bf16[1,64,8,128]{3,2,1,0:T(8,128)(2,1)S(1)}, bf16[1,64,8,128]{3,2,1,0:T(8,128)(2,1)S(1)}, u32[]{:S(2)}, u32[]{:S(2)}) collective-permute-start(bf16[1,64,8,128]{3,2,1,0:T(8,128)(2,1)S(1)} %get-tuple-element.45), channel_id=1, source_target_pairs={{0,3},{1,2},{2,1},{3,0},{4,7},{5,6},{6,5},{7,4},{8,11},{9,10},{10,... | collective-permute-start | bytes 393224 | tf_op jit(solution)/shard_map/ppermute | solution.py:28
  52.8 1.0 %collective-permute-start.7 = (bf16[1,64,8,128]{3,2,1,0:T(8,128)(2,1)S(1)}, bf16[1,64,8,128]{3,2,1,0:T(8,128)(2,1)S(1)}, u32[]{:S(2)}, u32[]{:S(2)}) collective-permute-start(bf16[1,64,8,128]{3,2,1,0:T(8,128)(2,1)S(1)} %get-tuple-element.42), channel_id=1, source_target_pairs={{0,2},{1,3},{2,0},{3,1},{4,6},{5,7},{6,4},{7,5},{8,10},{9,11},{10,... | collective-permute-start | bytes 393224 | tf_op jit(solution)/shard_map/ppermute | solution.py:28
  53.8 0.0 collective-permute-start.16
  53.8 0.0 collective-permute-done.13.refs_1_
  53.8 0.0 collective-permute-start.17
  53.8 2.9 %collective-permute-done.9.refs_4_ = bf16[1,64,8,128]{3,2,1,0:T(8,128)(2,1)S(1)} collective-permute-done((bf16[1,64,8,128]{3,2,1,0:T(8,128)(2,1)S(1)}, bf16[1,64,8,128]{3,2,1,0:T(8,128)(2,1)S(1)}, u32[]{:S(2)}, u32[]{:S(2)}) %collective-permute-start.9) | collective-permute-done | bytes 131104 | tf_op jit(solution)/shard_map/ppermute | solution.py:28
  56.7 0.6 collective-permute-start.14
  57.3 2.4 %collective-permute-done.7.refs_3_ = bf16[1,64,8,128]{3,2,1,0:T(8,128)(2,1)S(1)} collective-permute-done((bf16[1,64,8,128]{3,2,1,0:T(8,128)(2,1)S(1)}, bf16[1,64,8,128]{3,2,1,0:T(8,128)(2,1)S(1)}, u32[]{:S(2)}, u32[]{:S(2)}) %collective-permute-start.7) | collective-permute-done | bytes 131104 | tf_op jit(solution)/shard_map/ppermute | solution.py:28
  59.7 0.0 collective-permute-start.15
  59.7 0.0 collective-permute-done.5.refs_2_
  59.7 1.0 %collective-permute-start.11 = (bf16[1,64,8,128]{3,2,1,0:T(8,128)(2,1)S(1)}, bf16[1,64,8,128]{3,2,1,0:T(8,128)(2,1)S(1)}, u32[]{:S(2)}, u32[]{:S(2)}) collective-permute-start(bf16[1,64,8,128]{3,2,1,0:T(8,128)(2,1)S(1)} %get-tuple-element.48), channel_id=1, source_target_pairs={{0,2},{1,3},{2,0},{3,1},{4,6},{5,7},{6,4},{7,5},{8,10},{9,11},{10,... | collective-permute-start | bytes 393224 | tf_op jit(solution)/shard_map/ppermute | solution.py:28
  60.7 0.9 %store.1.old_ref = bf16[64,8,8,128]{3,2,1,0:T(8,128)(2,1)} custom-call(bf16[1,64,8,128]{3,2,1,0:T(8,128)(2,1)S(1)} %get-tuple-element.35.refs_0_, bf16[1,64,8,128]{3,2,1,0:T(8,128)(2,1)S(1)} %get-tuple-element.37.refs_1_, bf16[2,64,8,128]{3,2,1,0:T(8,128)(2,1)S(1)} %collective-permute-done.5.refs_2_, ...), custom_call_target="tpu_custom_call" | custom-call | tf_op jit(solution)/shard_map/store/pallas_call | solution.py:140
  61.6 2.4 %collective-permute-done.16.refs_6_ = bf16[2,256,128]{2,1,0:T(8,128)(2,1)S(1)} collective-permute-done((bf16[2,256,128]{2,1,0:T(8,128)(2,1)S(1)}, bf16[2,256,128]{2,1,0:T(8,128)(2,1)S(1)}, u32[]{:S(2)}, u32[]{:S(2)}) %collective-permute-start.16) | collective-permute-done | bytes 131104 | tf_op jit(solution)/shard_map/ppermute | solution.py:23
  64.0 0.0 collective-permute-done.17.refs_7_
  64.0 5.2 %collective-permute-done.14.refs_3_ = bf16[2,256,128]{2,1,0:T(8,128)(2,1)S(1)} collective-permute-done((bf16[2,256,128]{2,1,0:T(8,128)(2,1)S(1)}, bf16[2,256,128]{2,1,0:T(8,128)(2,1)S(1)}, u32[]{:S(2)}, u32[]{:S(2)}) %collective-permute-start.14) | collective-permute-done | bytes 131104 | tf_op jit(solution)/shard_map/ppermute | solution.py:23
  69.2 0.0 collective-permute-done.15.refs_4_
  69.2 0.0 collective-permute-done.11.refs_0_
  69.2 0.8 %finish.1 = (bf16[64,8,8,128]{3,2,1,0:T(8,128)(2,1)}, bf16[512,128]{1,0:T(8,128)(2,1)}, bf16[512,128]{1,0:T(8,128)(2,1)}) custom-call(bf16[64,8,8,128]{3,2,1,0:T(8,128)(2,1)} %store.1.old_ref, bf16[1,64,8,128]{3,2,1,0:T(8,128)(2,1)S(1)} %collective-permute-done.11.refs_0_, ...), custom_call_target="tpu_custom_call", output_to_operand_aliasing={{0}: (0, {})} | custom-call | tf_op jit(solution)/shard_map/finish/pallas_call | solution.py:174
  (1 shorter events, 0.0 us)
Async XLA Ops:
  2.2 23.8 %collective-permute-start = (bf16[2,2,64,8,128]{4,3,2,1,0:T(8,128)(2,1)S(1)}, bf16[2,2,64,8,128]{4,3,2,1,0:T(8,128)(2,1)S(1)}, u32[]{:S(2)}, u32[]{:S(2)}) collective-permute-start(bf16[2,2,64,8,128]{4,3,2,1,0:T(8,128)(2,1)S(1)} %get-tuple-element.33), channel_id=1, source_target_pairs={{0,1},{1,0},{2,3},{3,2},{4,5},{5,4},{6,7},{7,6},{8,9},{9,8},{10,11... | collective-permute-start | bytes 1572872 | tf_op jit(solution)/shard_map/ppermute | solution.py:28
  4.1 20.2 %collective-permute-start.3 = (bf16[2,256,128]{2,1,0:T(8,128)(2,1)S(1)}, bf16[2,256,128]{2,1,0:T(8,128)(2,1)S(1)}, u32[]{:S(2)}, u32[]{:S(2)}) collective-permute-start(bf16[2,256,128]{2,1,0:T(8,128)(2,1)S(1)} %get-tuple-element.36.refs_4_.refs_3_), channel_id=1, source_target_pairs={{0,8},{4,12},{8,16},{12,20},{16,24},{20,28},{24,0},{28,4},{1,9},{5... | collective-permute-start | bytes 393224 | tf_op jit(solution)/shard_map/ppermute | solution.py:23
  7.7 18.3 %collective-permute-start.4 = (bf16[2,256,128]{2,1,0:T(8,128)(2,1)S(1)}, bf16[2,256,128]{2,1,0:T(8,128)(2,1)S(1)}, u32[]{:S(2)}, u32[]{:S(2)}) collective-permute-start(bf16[2,256,128]{2,1,0:T(8,128)(2,1)S(1)} %get-tuple-element.36.refs_4_.refs_3_), channel_id=1, source_target_pairs={{0,4},{4,8},{8,12},{12,16},{16,20},{20,24},{24,28},{28,0},{1,5},{5... | collective-permute-start | bytes 393224 | tf_op jit(solution)/shard_map/ppermute | solution.py:23
  9.3 20.1 %collective-permute-start.1 = (bf16[2,256,128]{2,1,0:T(8,128)(2,1)S(1)}, bf16[2,256,128]{2,1,0:T(8,128)(2,1)S(1)}, u32[]{:S(2)}, u32[]{:S(2)}) collective-permute-start(bf16[2,256,128]{2,1,0:T(8,128)(2,1)S(1)} %get-tuple-element.34.refs_4_.refs_3_), channel_id=1, source_target_pairs={{0,8},{4,12},{8,16},{12,20},{16,24},{20,28},{24,0},{28,4},{1,9},{5... | collective-permute-start | bytes 393224 | tf_op jit(solution)/shard_map/ppermute | solution.py:23
  10.6 20.2 %collective-permute-start.2 = (bf16[2,256,128]{2,1,0:T(8,128)(2,1)S(1)}, bf16[2,256,128]{2,1,0:T(8,128)(2,1)S(1)}, u32[]{:S(2)}, u32[]{:S(2)}) collective-permute-start(bf16[2,256,128]{2,1,0:T(8,128)(2,1)S(1)} %get-tuple-element.34.refs_4_.refs_3_), channel_id=1, source_target_pairs={{0,4},{4,8},{8,12},{12,16},{16,20},{20,24},{24,28},{28,0},{1,5},{5... | collective-permute-start | bytes 393224 | tf_op jit(solution)/shard_map/ppermute | solution.py:23
  24.3 10.0 %collective-permute-start.10 = (bf16[1,2,64,8,128]{4,3,2,1,0:T(8,128)(2,1)S(1)}, bf16[1,2,64,8,128]{4,3,2,1,0:T(8,128)(2,1)S(1)}, u32[]{:S(2)}, u32[]{:S(2)}) collective-permute-start(bf16[1,2,64,8,128]{4,3,2,1,0:T(8,128)(2,1)S(1)} %get-tuple-element.46), channel_id=1, source_target_pairs={{0,2},{1,3},{2,0},{3,1},{4,6},{5,7},{6,4},{7,5},{8,10},{9,11},{10,... | collective-permute-start | bytes 786440 | tf_op jit(solution)/shard_map/ppermute | solution.py:28
  26.0 12.3 %collective-permute-start.12 = (bf16[1,2,64,8,128]{4,3,2,1,0:T(8,128)(2,1)S(1)}, bf16[1,2,64,8,128]{4,3,2,1,0:T(8,128)(2,1)S(1)}, u32[]{:S(2)}, u32[]{:S(2)}) collective-permute-start(bf16[1,2,64,8,128]{4,3,2,1,0:T(8,128)(2,1)S(1)} %get-tuple-element.49), channel_id=1, source_target_pairs={{0,3},{1,2},{2,1},{3,0},{4,7},{5,6},{6,5},{7,4},{8,11},{9,10},{10,... | collective-permute-start | bytes 786440 | tf_op jit(solution)/shard_map/ppermute | solution.py:28
  26.0 18.6 %collective-permute-start.6 = (bf16[1,2,64,8,128]{4,3,2,1,0:T(8,128)(2,1)S(1)}, bf16[1,2,64,8,128]{4,3,2,1,0:T(8,128)(2,1)S(1)}, u32[]{:S(2)}, u32[]{:S(2)}) collective-permute-start(bf16[1,2,64,8,128]{4,3,2,1,0:T(8,128)(2,1)S(1)} %get-tuple-element.40), channel_id=1, source_target_pairs={{0,2},{1,3},{2,0},{3,1},{4,6},{5,7},{6,4},{7,5},{8,10},{9,11},{10,... | collective-permute-start | bytes 786440 | tf_op jit(solution)/shard_map/ppermute | solution.py:28
  29.4 19.7 %collective-permute-start.8 = (bf16[1,2,64,8,128]{4,3,2,1,0:T(8,128)(2,1)S(1)}, bf16[1,2,64,8,128]{4,3,2,1,0:T(8,128)(2,1)S(1)}, u32[]{:S(2)}, u32[]{:S(2)}) collective-permute-start(bf16[1,2,64,8,128]{4,3,2,1,0:T(8,128)(2,1)S(1)} %get-tuple-element.43), channel_id=1, source_target_pairs={{0,3},{1,2},{2,1},{3,0},{4,7},{5,6},{6,5},{7,4},{8,11},{9,10},{10,... | collective-permute-start | bytes 786440 | tf_op jit(solution)/shard_map/ppermute | solution.py:28
  33.7 26.0 %collective-permute-start.5 = (bf16[2,64,8,128]{3,2,1,0:T(8,128)(2,1)S(1)}, bf16[2,64,8,128]{3,2,1,0:T(8,128)(2,1)S(1)}, u32[]{:S(2)}, u32[]{:S(2)}) collective-permute-start(bf16[2,64,8,128]{3,2,1,0:T(8,128)(2,1)S(1)} %pad_maximum_fusion), channel_id=1, source_target_pairs={{0,1},{1,0},{2,3},{3,2},{4,5},{5,4},{6,7},{7,6},{8,9},{9,8},{10,11... | collective-permute-start | bytes 786440 | tf_op jit(solution)/shard_map/ppermute | solution.py:28
  40.0 13.8 %collective-permute-start.13 = (bf16[1,64,8,128]{3,2,1,0:T(8,128)(2,1)S(1)}, bf16[1,64,8,128]{3,2,1,0:T(8,128)(2,1)S(1)}, u32[]{:S(2)}, u32[]{:S(2)}) collective-permute-start(bf16[1,64,8,128]{3,2,1,0:T(8,128)(2,1)S(1)} %get-tuple-element.51), channel_id=1, source_target_pairs={{0,3},{1,2},{2,1},{3,0},{4,7},{5,6},{6,5},{7,4},{8,11},{9,10},{10,... | collective-permute-start | bytes 393224 | tf_op jit(solution)/shard_map/ppermute | solution.py:28
  50.8 5.9 %collective-permute-start.9 = (bf16[1,64,8,128]{3,2,1,0:T(8,128)(2,1)S(1)}, bf16[1,64,8,128]{3,2,1,0:T(8,128)(2,1)S(1)}, u32[]{:S(2)}, u32[]{:S(2)}) collective-permute-start(bf16[1,64,8,128]{3,2,1,0:T(8,128)(2,1)S(1)} %get-tuple-element.45), channel_id=1, source_target_pairs={{0,3},{1,2},{2,1},{3,0},{4,7},{5,6},{6,5},{7,4},{8,11},{9,10},{10,... | collective-permute-start | bytes 393224 | tf_op jit(solution)/shard_map/ppermute | solution.py:28
  52.8 6.9 %collective-permute-start.7 = (bf16[1,64,8,128]{3,2,1,0:T(8,128)(2,1)S(1)}, bf16[1,64,8,128]{3,2,1,0:T(8,128)(2,1)S(1)}, u32[]{:S(2)}, u32[]{:S(2)}) collective-permute-start(bf16[1,64,8,128]{3,2,1,0:T(8,128)(2,1)S(1)} %get-tuple-element.42), channel_id=1, source_target_pairs={{0,2},{1,3},{2,0},{3,1},{4,6},{5,7},{6,4},{7,5},{8,10},{9,11},{10,... | collective-permute-start | bytes 393224 | tf_op jit(solution)/shard_map/ppermute | solution.py:28
  53.8 10.2 %collective-permute-start.16 = (bf16[2,256,128]{2,1,0:T(8,128)(2,1)S(1)}, bf16[2,256,128]{2,1,0:T(8,128)(2,1)S(1)}, u32[]{:S(2)}, u32[]{:S(2)}) collective-permute-start(bf16[2,256,128]{2,1,0:T(8,128)(2,1)S(1)} %get-tuple-element.56), channel_id=1, source_target_pairs={{0,24},{4,28},{8,0},{12,4},{16,8},{20,12},{24,16},{28,20},{1,25},{... | collective-permute-start | bytes 393224 | tf_op jit(solution)/shard_map/ppermute | solution.py:23
  53.8 10.2 %collective-permute-start.17 = (bf16[2,256,128]{2,1,0:T(8,128)(2,1)S(1)}, bf16[2,256,128]{2,1,0:T(8,128)(2,1)S(1)}, u32[]{:S(2)}, u32[]{:S(2)}) collective-permute-start(bf16[2,256,128]{2,1,0:T(8,128)(2,1)S(1)} %get-tuple-element.57), channel_id=1, source_target_pairs={{0,28},{4,0},{8,4},{12,8},{16,12},{20,16},{24,20},{28,24},{1,29},{... | collective-permute-start | bytes 393224 | tf_op jit(solution)/shard_map/ppermute | solution.py:23
  56.7 12.5 %collective-permute-start.14 = (bf16[2,256,128]{2,1,0:T(8,128)(2,1)S(1)}, bf16[2,256,128]{2,1,0:T(8,128)(2,1)S(1)}, u32[]{:S(2)}, u32[]{:S(2)}) collective-permute-start(bf16[2,256,128]{2,1,0:T(8,128)(2,1)S(1)} %get-tuple-element.53), channel_id=1, source_target_pairs={{0,24},{4,28},{8,0},{12,4},{16,8},{20,12},{24,16},{28,20},{1,25},{... | collective-permute-start | bytes 393224 | tf_op jit(solution)/shard_map/ppermute | solution.py:23
  59.7 9.5 %collective-permute-start.15 = (bf16[2,256,128]{2,1,0:T(8,128)(2,1)S(1)}, bf16[2,256,128]{2,1,0:T(8,128)(2,1)S(1)}, u32[]{:S(2)}, u32[]{:S(2)}) collective-permute-start(bf16[2,256,128]{2,1,0:T(8,128)(2,1)S(1)} %get-tuple-element.54), channel_id=1, source_target_pairs={{0,28},{4,0},{8,4},{12,8},{16,12},{20,16},{24,20},{28,24},{1,29},{... | collective-permute-start | bytes 393224 | tf_op jit(solution)/shard_map/ppermute | solution.py:23
  59.7 9.5 %collective-permute-start.11 = (bf16[1,64,8,128]{3,2,1,0:T(8,128)(2,1)S(1)}, bf16[1,64,8,128]{3,2,1,0:T(8,128)(2,1)S(1)}, u32[]{:S(2)}, u32[]{:S(2)}) collective-permute-start(bf16[1,64,8,128]{3,2,1,0:T(8,128)(2,1)S(1)} %get-tuple-element.48), channel_id=1, source_target_pairs={{0,2},{1,3},{2,0},{3,1},{4,6},{5,7},{6,4},{7,5},{8,10},{9,11},{10,... | collective-permute-start | bytes 393224 | tf_op jit(solution)/shard_map/ppermute | solution.py:28

commit v2 on v1

--- a/solution.py
+++ b/solution.py
@@ -225,6 +225,13 @@
         n, t = piece
         return pair_refs[n][where[n], which, t : t + tokens].reshape(block_rows, width)
 
+    def value_dots(piece):
+        do = part(piece, 1)
+        return [
+            lax.dot_general(window[1], do, NT, preferred_element_type=jnp.float32)
+            for window in windows
+        ]
+
     def scored(piece):
         n, t = piece
         q = part(piece, 0)
@@ -238,16 +245,20 @@
                 s = jnp.where(key <= token, s, -jnp.inf)
             scores.append(s)
             tops.append(jnp.max(s, axis=0, keepdims=True) - bias[j])
-        return scores, jnp.maximum(jnp.maximum(tops[0], tops[1]), tops[2]) * to_exp2
+        dps = value_dots(piece) if count == 1 else None
+        return scores, dps, jnp.maximum(jnp.maximum(tops[0], tops[1]), tops[2]) * to_exp2
 
     ahead = scored(pieces[0])
     for step, piece in enumerate(pieces):
-        scores, top = ahead
+        scores, dps, top = ahead
         q, do = part(piece, 0), part(piece, 1)
         weights, dprobs, total, dtotal = [], [], 0.0, 0.0
         for j, window in enumerate(windows):
             e = jnp.exp2(scores[j] * to_exp2 - (top + bias[j]))
-            dp = lax.dot_general(window[1], do, NT, preferred_element_type=jnp.float32)
+            if dps is None:
+                dp = lax.dot_general(window[1], do, NT, preferred_element_type=jnp.float32)
+            else:
+                dp = dps[j]
             total = total + jnp.sum(e, axis=0, keepdims=True)
             dtotal = dtotal + jnp.sum(e * dp, axis=0, keepdims=True)
             weights.append(e)

time: 70.2 us -> 70.1 us (level)
  transfers between devices with their start and end apart: 18 -> 18, of which waited for: 8 -> 8; matrix products, arithmetic and copies ran while one was open for 0% -> 0% of each run, Pallas kernels for 21% -> 20%
where the time goes in v2:
time: 70.1 us; the launch traced here: 69.9 us
  waiting for transfers between devices  32.4 us (46%)
  starting transfers between devices  20.1 us (29%)
  Pallas kernels  16.7 us (24%)
  between operations  0.71 us (1%)
    ppermute x8, waiting for transfers between devices, shifted(): return lax.ppermute(value, SEQ, pairs)  18.8 us
    ppermute x10, waiting for transfers between devices, swapped(): lax.ppermute(value, 'head', [(i, i ^ distance) for i in range(peers)])  13.6 us
    pallas_call x6, Pallas kernels, group_grads(): pl.pallas_call(functools.partial(grads_kernel, where, distances, sums is...  12.1 us
    ppermute x10, starting transfers between devices, swapped(): lax.ppermute(value, 'head', [(i, i ^ distance) for i in range(peers)])  10.6 us
    ppermute x8, starting transfers between devices, shifted(): return lax.ppermute(value, SEQ, pairs)  9.58 us
    pallas_call x1, Pallas kernels, pack(): pl.pallas_call(functools.partial(pack_kernel, parts, kv_heads), in_specs=...  1.6 us
  transfers between devices with their start and end apart: 18, of which 8 were waited for; matrix products, arithmetic and copies ran while one was open for 0% of the time, Pallas kernels for 20%

profile of v2, /device:TPU:0, one launch (start us, length us, event | category | flops | bytes accessed | tf_op | source)
XLA Modules:
  0.0 69.9 jit_solution(167567750058783897)
XLA Ops:
  0.6 1.6 %pack.1 = (bf16[2,2,64,8,128]{4,3,2,1,0:T(8,128)(2,1)S(1)}, bf16[2,2,64,8,128]{4,3,2,1,0:T(8,128)(2,1)S(1)}, bf16[1,2,64,8,128]{4,3,2,1,0:T(8,128)(2,1)S(1)}, bf16[1,2,64,8,128]{4,3,2,1,0:T(8,128)(2,1)S(1)}) custom-call(bf16[64,8,8,128]{3,2,1,0:T(8,128)(2,1)} %bitcast.8, bf16[64,8,8,128]{3,2,1,0:T(8,128)(2,1)} %bitcast.10), custom_call_target="tpu_custom_call" | custom-call | tf_op jit(solution)/shard_map/pack/pallas_call | solution.py:79
  2.2 0.6 collective-permute-start
  2.8 1.3 %first.1 = (bf16[2,256,128]{2,1,0:T(8,128)(2,1)S(1)}, bf16[2,256,128]{2,1,0:T(8,128)(2,1)S(1)}, bf16[1,2,64,8,128]{4,3,2,1,0:T(8,128)(2,1)S(1)}, bf16[1,2,64,8,128]{4,3,2,1,0:T(8,128)(2,1)S(1)}) custom-call(bf16[512,128]{1,0:T(8,128)(2,1)} %bitcast.12, bf16[512,128]{1,0:T(8,128)(2,1)} %bitcast.13, bf16[64,8,8,128]{3,2,1,0:T(8,128)(2,1)} %bitcast.9, ...), custom_call_target="tpu_custom_call" | custom-call | tf_op jit(solution)/shard_map/first/pallas_call | solution.py:95
  4.1 3.6 %collective-permute-start.3 = (bf16[2,256,128]{2,1,0:T(8,128)(2,1)S(1)}, bf16[2,256,128]{2,1,0:T(8,128)(2,1)S(1)}, u32[]{:S(2)}, u32[]{:S(2)}) collective-permute-start(bf16[2,256,128]{2,1,0:T(8,128)(2,1)S(1)} %get-tuple-element.36.refs_4_.refs_3_), channel_id=1, source_target_pairs={{0,8},{4,12},{8,16},{12,20},{16,24},{20,28},{24,0},{28,4},{1,9},{5... | collective-permute-start | bytes 393224 | tf_op jit(solution)/shard_map/ppermute | solution.py:23
  7.7 1.6 %collective-permute-start.4 = (bf16[2,256,128]{2,1,0:T(8,128)(2,1)S(1)}, bf16[2,256,128]{2,1,0:T(8,128)(2,1)S(1)}, u32[]{:S(2)}, u32[]{:S(2)}) collective-permute-start(bf16[2,256,128]{2,1,0:T(8,128)(2,1)S(1)} %get-tuple-element.36.refs_4_.refs_3_), channel_id=1, source_target_pairs={{0,4},{4,8},{8,12},{12,16},{16,20},{20,24},{24,28},{28,0},{1,5},{5... | collective-permute-start | bytes 393224 | tf_op jit(solution)/shard_map/ppermute | solution.py:23
  9.3 1.3 %collective-permute-start.1 = (bf16[2,256,128]{2,1,0:T(8,128)(2,1)S(1)}, bf16[2,256,128]{2,1,0:T(8,128)(2,1)S(1)}, u32[]{:S(2)}, u32[]{:S(2)}) collective-permute-start(bf16[2,256,128]{2,1,0:T(8,128)(2,1)S(1)} %get-tuple-element.34.refs_4_.refs_3_), channel_id=1, source_target_pairs={{0,8},{4,12},{8,16},{12,20},{16,24},{20,28},{24,0},{28,4},{1,9},{5... | collective-permute-start | bytes 393224 | tf_op jit(solution)/shard_map/ppermute | solution.py:23
  10.6 2.5 %collective-permute-start.2 = (bf16[2,256,128]{2,1,0:T(8,128)(2,1)S(1)}, bf16[2,256,128]{2,1,0:T(8,128)(2,1)S(1)}, u32[]{:S(2)}, u32[]{:S(2)}) collective-permute-start(bf16[2,256,128]{2,1,0:T(8,128)(2,1)S(1)} %get-tuple-element.34.refs_4_.refs_3_), channel_id=1, source_target_pairs={{0,4},{4,8},{8,12},{12,16},{16,20},{20,24},{24,28},{28,0},{1,5},{5... | collective-permute-start | bytes 393224 | tf_op jit(solution)/shard_map/ppermute | solution.py:23
  13.1 11.2 %collective-permute-done.3.refs_2_.refs_1_ = bf16[2,256,128]{2,1,0:T(8,128)(2,1)S(1)} collective-permute-done((bf16[2,256,128]{2,1,0:T(8,128)(2,1)S(1)}, bf16[2,256,128]{2,1,0:T(8,128)(2,1)S(1)}, u32[]{:S(2)}, u32[]{:S(2)}) %collective-permute-start.3) | collective-permute-done | bytes 131104 | tf_op jit(solution)/shard_map/ppermute | solution.py:23
  24.3 1.8 %collective-permute-start.10 = (bf16[1,2,64,8,128]{4,3,2,1,0:T(8,128)(2,1)S(1)}, bf16[1,2,64,8,128]{4,3,2,1,0:T(8,128)(2,1)S(1)}, u32[]{:S(2)}, u32[]{:S(2)}) collective-permute-start(bf16[1,2,64,8,128]{4,3,2,1,0:T(8,128)(2,1)S(1)} %get-tuple-element.46), channel_id=1, source_target_pairs={{0,2},{1,3},{2,0},{3,1},{4,6},{5,7},{6,4},{7,5},{8,10},{9,11},{10,... | collective-permute-start | bytes 786440 | tf_op jit(solution)/shard_map/ppermute | solution.py:28
  26.0 0.0 collective-permute-done.4.refs_3_.refs_2_
  26.0 0.0 collective-permute-start.12
  26.0 0.0 collective-permute-done.refs_1_
  26.0 0.5 collective-permute-start.6
  26.5 2.9 %grads.7 = (bf16[1,64,8,128]{3,2,1,0:T(8,128)(2,1)S(1)}, bf16[1,64,8,128]{3,2,1,0:T(8,128)(2,1)S(1)}, f32[3,2,256,128]{3,2,1,0:T(8,128)S(1)}) custom-call(bf16[2,2,64,8,128]{4,3,2,1,0:T(8,128)(2,1)S(1)} %get-tuple-element.32.refs_0_, bf16[2,2,64,8,128]{4,3,2,1,0:T(8,128)(2,1)S(1)} %collective-permute-done.refs_1_, ...), custom_call_target="tpu_custom_call" | custom-call | flops 1006632960 | bytes 786432 | tf_op jit(solution)/shard_map/grads/pallas_call | solution.py:307
  29.4 0.0 collective-permute-done.1.refs_2_.refs_1_
  29.4 1.3 %collective-permute-start.8 = (bf16[1,2,64,8,128]{4,3,2,1,0:T(8,128)(2,1)S(1)}, bf16[1,2,64,8,128]{4,3,2,1,0:T(8,128)(2,1)S(1)}, u32[]{:S(2)}, u32[]{:S(2)}) collective-permute-start(bf16[1,2,64,8,128]{4,3,2,1,0:T(8,128)(2,1)S(1)} %get-tuple-element.43), channel_id=1, source_target_pairs={{0,3},{1,2},{2,1},{3,0},{4,7},{5,6},{6,5},{7,4},{8,11},{9,10},{10,... | collective-permute-start | bytes 786440 | tf_op jit(solution)/shard_map/ppermute | solution.py:28
  30.7 0.0 collective-permute-done.2.refs_3_.refs_2_
  30.8 2.9 %grads.6 = (bf16[1,64,8,128]{3,2,1,0:T(8,128)(2,1)S(1)}, bf16[1,64,8,128]{3,2,1,0:T(8,128)(2,1)S(1)}, f32[3,2,256,128]{3,2,1,0:T(8,128)S(1)}) custom-call(bf16[2,2,64,8,128]{4,3,2,1,0:T(8,128)(2,1)S(1)} %get-tuple-element.32.refs_0_, bf16[2,2,64,8,128]{4,3,2,1,0:T(8,128)(2,1)S(1)} %collective-permute-done.refs_1_, ...), custom_call_target="tpu_custom_call" | custom-call | flops 1006632960 | bytes 786432 | tf_op jit(solution)/shard_map/grads/pallas_call | solution.py:307
  33.7 0.5 collective-permute-start.5
  34.2 0.0 collective-permute-done.10.refs_0_
  34.2 1.6 %grads.10 = (bf16[1,64,8,128]{3,2,1,0:T(8,128)(2,1)S(1)}, f32[3,2,256,128]{3,2,1,0:T(8,128)S(1)}) custom-call(bf16[1,2,64,8,128]{4,3,2,1,0:T(8,128)(2,1)S(1)} %collective-permute-done.10.refs_0_, bf16[2,256,128]{2,1,0:T(8,128)(2,1)S(1)} %collective-permute-done.3.refs_2_.refs_1_, bf16[2,256,128]{2,1,0:T(8,128)(2,1)S(1)} %collective-permute-done.4.refs_3_.refs_2_, ...), custom_call_target="tpu_custom_call" | custom-call | flops 503316480 | bytes 393216 | tf_op jit(solution)/shard_map/grads/pallas_call | solution.py:307
  35.8 2.5 %collective-permute-done.12.refs_0_ = bf16[1,2,64,8,128]{4,3,2,1,0:T(8,128)(2,1)S(1)} collective-permute-done((bf16[1,2,64,8,128]{4,3,2,1,0:T(8,128)(2,1)S(1)}, bf16[1,2,64,8,128]{4,3,2,1,0:T(8,128)(2,1)S(1)}, u32[]{:S(2)}, u32[]{:S(2)}) %collective-permute-start.12) | collective-permute-done | bytes 262176 | tf_op jit(solution)/shard_map/ppermute | solution.py:28
  38.3 1.6 %grads.11 = (bf16[1,64,8,128]{3,2,1,0:T(8,128)(2,1)S(1)}, bf16[2,256,128]{2,1,0:T(8,128)(2,1)S(1)}, bf16[2,256,128]{2,1,0:T(8,128)(2,1)S(1)}, f32[2,256,128]{2,1,0:T(8,128)S(1)}) custom-call(bf16[1,2,64,8,128]{4,3,2,1,0:T(8,128)(2,1)S(1)} %collective-permute-done.12.refs_0_, bf16[2,256,128]{2,1,0:T(8,128)(2,1)S(1)} %collective-permute-done.3.refs_2_.refs_1_, ...), custom_call_target="tpu_custom_call" | custom-call | flops 503316480 | bytes 393216 | tf_op jit(solution)/shard_map/grads/pallas_call | solution.py:307
  39.9 2.0 %collective-permute-start.13 = (bf16[1,64,8,128]{3,2,1,0:T(8,128)(2,1)S(1)}, bf16[1,64,8,128]{3,2,1,0:T(8,128)(2,1)S(1)}, u32[]{:S(2)}, u32[]{:S(2)}) collective-permute-start(bf16[1,64,8,128]{3,2,1,0:T(8,128)(2,1)S(1)} %get-tuple-element.51), channel_id=1, source_target_pairs={{0,3},{1,2},{2,1},{3,0},{4,7},{5,6},{6,5},{7,4},{8,11},{9,10},{10,... | collective-permute-start | bytes 393224 | tf_op jit(solution)/shard_map/ppermute | solution.py:28
  41.9 2.8 %collective-permute-done.6.refs_0_ = bf16[1,2,64,8,128]{4,3,2,1,0:T(8,128)(2,1)S(1)} collective-permute-done((bf16[1,2,64,8,128]{4,3,2,1,0:T(8,128)(2,1)S(1)}, bf16[1,2,64,8,128]{4,3,2,1,0:T(8,128)(2,1)S(1)}, u32[]{:S(2)}, u32[]{:S(2)}) %collective-permute-start.6) | collective-permute-done | bytes 262176 | tf_op jit(solution)/shard_map/ppermute | solution.py:28
  44.7 1.6 %grads.8 = (bf16[1,64,8,128]{3,2,1,0:T(8,128)(2,1)S(1)}, f32[3,2,256,128]{3,2,1,0:T(8,128)S(1)}) custom-call(bf16[1,2,64,8,128]{4,3,2,1,0:T(8,128)(2,1)S(1)} %collective-permute-done.6.refs_0_, bf16[2,256,128]{2,1,0:T(8,128)(2,1)S(1)} %collective-permute-done.1.refs_2_.refs_1_, bf16[2,256,128]{2,1,0:T(8,128)(2,1)S(1)} %collective-permute-done.2.refs_3_.refs_2_, ...), custom_call_target="tpu_custom_call" | custom-call | flops 503316480 | bytes 393216 | tf_op jit(solution)/shard_map/grads/pallas_call | solution.py:307
  46.2 2.9 %collective-permute-done.8.refs_0_ = bf16[1,2,64,8,128]{4,3,2,1,0:T(8,128)(2,1)S(1)} collective-permute-done((bf16[1,2,64,8,128]{4,3,2,1,0:T(8,128)(2,1)S(1)}, bf16[1,2,64,8,128]{4,3,2,1,0:T(8,128)(2,1)S(1)}, u32[]{:S(2)}, u32[]{:S(2)}) %collective-permute-start.8) | collective-permute-done | bytes 262176 | tf_op jit(solution)/shard_map/ppermute | solution.py:28
  49.2 1.6 %grads.9 = (bf16[1,64,8,128]{3,2,1,0:T(8,128)(2,1)S(1)}, bf16[2,256,128]{2,1,0:T(8,128)(2,1)S(1)}, bf16[2,256,128]{2,1,0:T(8,128)(2,1)S(1)}, f32[2,256,128]{2,1,0:T(8,128)S(1)}) custom-call(bf16[1,2,64,8,128]{4,3,2,1,0:T(8,128)(2,1)S(1)} %collective-permute-done.8.refs_0_, bf16[2,256,128]{2,1,0:T(8,128)(2,1)S(1)} %collective-permute-done.1.refs_2_.refs_1_, ...), custom_call_target="tpu_custom_call" | custom-call | flops 503316480 | bytes 393216 | tf_op jit(solution)/shard_map/grads/pallas_call | solution.py:307
  50.7 2.0 %collective-permute-start.9 = (bf16[1,64,8,128]{3,2,1,0:T(8,128)(2,1)S(1)}, bf16[1,64,8,128]{3,2,1,0:T(8,128)(2,1)S(1)}, u32[]{:S(2)}, u32[]{:S(2)}) collective-permute-start(bf16[1,64,8,128]{3,2,1,0:T(8,128)(2,1)S(1)} %get-tuple-element.45), channel_id=1, source_target_pairs={{0,3},{1,2},{2,1},{3,0},{4,7},{5,6},{6,5},{7,4},{8,11},{9,10},{10,... | collective-permute-start | bytes 393224 | tf_op jit(solution)/shard_map/ppermute | solution.py:28
  52.7 1.0 %collective-permute-start.7 = (bf16[1,64,8,128]{3,2,1,0:T(8,128)(2,1)S(1)}, bf16[1,64,8,128]{3,2,1,0:T(8,128)(2,1)S(1)}, u32[]{:S(2)}, u32[]{:S(2)}) collective-permute-start(bf16[1,64,8,128]{3,2,1,0:T(8,128)(2,1)S(1)} %get-tuple-element.42), channel_id=1, source_target_pairs={{0,2},{1,3},{2,0},{3,1},{4,6},{5,7},{6,4},{7,5},{8,10},{9,11},{10,... | collective-permute-start | bytes 393224 | tf_op jit(solution)/shard_map/ppermute | solution.py:28
  53.7 0.0 collective-permute-start.16
  53.7 0.0 collective-permute-done.13.refs_1_
  53.7 0.0 collective-permute-start.17
  53.7 2.9 %collective-permute-done.9.refs_4_ = bf16[1,64,8,128]{3,2,1,0:T(8,128)(2,1)S(1)} collective-permute-done((bf16[1,64,8,128]{3,2,1,0:T(8,128)(2,1)S(1)}, bf16[1,64,8,128]{3,2,1,0:T(8,128)(2,1)S(1)}, u32[]{:S(2)}, u32[]{:S(2)}) %collective-permute-start.9) | collective-permute-done | bytes 131104 | tf_op jit(solution)/shard_map/ppermute | solution.py:28
  56.6 0.6 collective-permute-start.14
  57.2 2.4 %collective-permute-done.7.refs_3_ = bf16[1,64,8,128]{3,2,1,0:T(8,128)(2,1)S(1)} collective-permute-done((bf16[1,64,8,128]{3,2,1,0:T(8,128)(2,1)S(1)}, bf16[1,64,8,128]{3,2,1,0:T(8,128)(2,1)S(1)}, u32[]{:S(2)}, u32[]{:S(2)}) %collective-permute-start.7) | collective-permute-done | bytes 131104 | tf_op jit(solution)/shard_map/ppermute | solution.py:28
  59.6 0.0 collective-permute-start.15
  59.6 0.0 collective-permute-done.5.refs_2_
  59.6 1.0 %collective-permute-start.11 = (bf16[1,64,8,128]{3,2,1,0:T(8,128)(2,1)S(1)}, bf16[1,64,8,128]{3,2,1,0:T(8,128)(2,1)S(1)}, u32[]{:S(2)}, u32[]{:S(2)}) collective-permute-start(bf16[1,64,8,128]{3,2,1,0:T(8,128)(2,1)S(1)} %get-tuple-element.48), channel_id=1, source_target_pairs={{0,2},{1,3},{2,0},{3,1},{4,6},{5,7},{6,4},{7,5},{8,10},{9,11},{10,... | collective-permute-start | bytes 393224 | tf_op jit(solution)/shard_map/ppermute | solution.py:28
  60.6 0.9 %store.1.old_ref = bf16[64,8,8,128]{3,2,1,0:T(8,128)(2,1)} custom-call(bf16[1,64,8,128]{3,2,1,0:T(8,128)(2,1)S(1)} %get-tuple-element.35.refs_0_, bf16[1,64,8,128]{3,2,1,0:T(8,128)(2,1)S(1)} %get-tuple-element.37.refs_1_, bf16[2,64,8,128]{3,2,1,0:T(8,128)(2,1)S(1)} %collective-permute-done.5.refs_2_, ...), custom_call_target="tpu_custom_call" | custom-call | tf_op jit(solution)/shard_map/store/pallas_call | solution.py:140
  61.5 2.4 %collective-permute-done.16.refs_6_ = bf16[2,256,128]{2,1,0:T(8,128)(2,1)S(1)} collective-permute-done((bf16[2,256,128]{2,1,0:T(8,128)(2,1)S(1)}, bf16[2,256,128]{2,1,0:T(8,128)(2,1)S(1)}, u32[]{:S(2)}, u32[]{:S(2)}) %collective-permute-start.16) | collective-permute-done | bytes 131104 | tf_op jit(solution)/shard_map/ppermute | solution.py:23
  63.9 0.0 collective-permute-done.17.refs_7_
  63.9 5.2 %collective-permute-done.14.refs_3_ = bf16[2,256,128]{2,1,0:T(8,128)(2,1)S(1)} collective-permute-done((bf16[2,256,128]{2,1,0:T(8,128)(2,1)S(1)}, bf16[2,256,128]{2,1,0:T(8,128)(2,1)S(1)}, u32[]{:S(2)}, u32[]{:S(2)}) %collective-permute-start.14) | collective-permute-done | bytes 131104 | tf_op jit(solution)/shard_map/ppermute | solution.py:23
  69.1 0.0 collective-permute-done.15.refs_4_
  69.1 0.0 collective-permute-done.11.refs_0_
  69.1 0.8 %finish.1 = (bf16[64,8,8,128]{3,2,1,0:T(8,128)(2,1)}, bf16[512,128]{1,0:T(8,128)(2,1)}, bf16[512,128]{1,0:T(8,128)(2,1)}) custom-call(bf16[64,8,8,128]{3,2,1,0:T(8,128)(2,1)} %store.1.old_ref, bf16[1,64,8,128]{3,2,1,0:T(8,128)(2,1)S(1)} %collective-permute-done.11.refs_0_, ...), custom_call_target="tpu_custom_call", output_to_operand_aliasing={{0}: (0, {})} | custom-call | tf_op jit(solution)/shard_map/finish/pallas_call | solution.py:174
  (1 shorter events, 0.0 us)
Async XLA Ops:
  2.2 23.8 %collective-permute-start = (bf16[2,2,64,8,128]{4,3,2,1,0:T(8,128)(2,1)S(1)}, bf16[2,2,64,8,128]{4,3,2,1,0:T(8,128)(2,1)S(1)}, u32[]{:S(2)}, u32[]{:S(2)}) collective-permute-start(bf16[2,2,64,8,128]{4,3,2,1,0:T(8,128)(2,1)S(1)} %get-tuple-element.33), channel_id=1, source_target_pairs={{0,1},{1,0},{2,3},{3,2},{4,5},{5,4},{6,7},{7,6},{8,9},{9,8},{10,11... | collective-permute-start | bytes 1572872 | tf_op jit(solution)/shard_map/ppermute | solution.py:28
  4.1 20.2 %collective-permute-start.3 = (bf16[2,256,128]{2,1,0:T(8,128)(2,1)S(1)}, bf16[2,256,128]{2,1,0:T(8,128)(2,1)S(1)}, u32[]{:S(2)}, u32[]{:S(2)}) collective-permute-start(bf16[2,256,128]{2,1,0:T(8,128)(2,1)S(1)} %get-tuple-element.36.refs_4_.refs_3_), channel_id=1, source_target_pairs={{0,8},{4,12},{8,16},{12,20},{16,24},{20,28},{24,0},{28,4},{1,9},{5... | collective-permute-start | bytes 393224 | tf_op jit(solution)/shard_map/ppermute | solution.py:23
  7.7 18.3 %collective-permute-start.4 = (bf16[2,256,128]{2,1,0:T(8,128)(2,1)S(1)}, bf16[2,256,128]{2,1,0:T(8,128)(2,1)S(1)}, u32[]{:S(2)}, u32[]{:S(2)}) collective-permute-start(bf16[2,256,128]{2,1,0:T(8,128)(2,1)S(1)} %get-tuple-element.36.refs_4_.refs_3_), channel_id=1, source_target_pairs={{0,4},{4,8},{8,12},{12,16},{16,20},{20,24},{24,28},{28,0},{1,5},{5... | collective-permute-start | bytes 393224 | tf_op jit(solution)/shard_map/ppermute | solution.py:23
  9.3 20.1 %collective-permute-start.1 = (bf16[2,256,128]{2,1,0:T(8,128)(2,1)S(1)}, bf16[2,256,128]{2,1,0:T(8,128)(2,1)S(1)}, u32[]{:S(2)}, u32[]{:S(2)}) collective-permute-start(bf16[2,256,128]{2,1,0:T(8,128)(2,1)S(1)} %get-tuple-element.34.refs_4_.refs_3_), channel_id=1, source_target_pairs={{0,8},{4,12},{8,16},{12,20},{16,24},{20,28},{24,0},{28,4},{1,9},{5... | collective-permute-start | bytes 393224 | tf_op jit(solution)/shard_map/ppermute | solution.py:23
  10.6 20.2 %collective-permute-start.2 = (bf16[2,256,128]{2,1,0:T(8,128)(2,1)S(1)}, bf16[2,256,128]{2,1,0:T(8,128)(2,1)S(1)}, u32[]{:S(2)}, u32[]{:S(2)}) collective-permute-start(bf16[2,256,128]{2,1,0:T(8,128)(2,1)S(1)} %get-tuple-element.34.refs_4_.refs_3_), channel_id=1, source_target_pairs={{0,4},{4,8},{8,12},{12,16},{16,20},{20,24},{24,28},{28,0},{1,5},{5... | collective-permute-start | bytes 393224 | tf_op jit(solution)/shard_map/ppermute | solution.py:23
  24.3 10.0 %collective-permute-start.10 = (bf16[1,2,64,8,128]{4,3,2,1,0:T(8,128)(2,1)S(1)}, bf16[1,2,64,8,128]{4,3,2,1,0:T(8,128)(2,1)S(1)}, u32[]{:S(2)}, u32[]{:S(2)}) collective-permute-start(bf16[1,2,64,8,128]{4,3,2,1,0:T(8,128)(2,1)S(1)} %get-tuple-element.46), channel_id=1, source_target_pairs={{0,2},{1,3},{2,0},{3,1},{4,6},{5,7},{6,4},{7,5},{8,10},{9,11},{10,... | collective-permute-start | bytes 786440 | tf_op jit(solution)/shard_map/ppermute | solution.py:28
  26.0 12.3 %collective-permute-start.12 = (bf16[1,2,64,8,128]{4,3,2,1,0:T(8,128)(2,1)S(1)}, bf16[1,2,64,8,128]{4,3,2,1,0:T(8,128)(2,1)S(1)}, u32[]{:S(2)}, u32[]{:S(2)}) collective-permute-start(bf16[1,2,64,8,128]{4,3,2,1,0:T(8,128)(2,1)S(1)} %get-tuple-element.49), channel_id=1, source_target_pairs={{0,3},{1,2},{2,1},{3,0},{4,7},{5,6},{6,5},{7,4},{8,11},{9,10},{10,... | collective-permute-start | bytes 786440 | tf_op jit(solution)/shard_map/ppermute | solution.py:28
  26.0 18.6 %collective-permute-start.6 = (bf16[1,2,64,8,128]{4,3,2,1,0:T(8,128)(2,1)S(1)}, bf16[1,2,64,8,128]{4,3,2,1,0:T(8,128)(2,1)S(1)}, u32[]{:S(2)}, u32[]{:S(2)}) collective-permute-start(bf16[1,2,64,8,128]{4,3,2,1,0:T(8,128)(2,1)S(1)} %get-tuple-element.40), channel_id=1, source_target_pairs={{0,2},{1,3},{2,0},{3,1},{4,6},{5,7},{6,4},{7,5},{8,10},{9,11},{10,... | collective-permute-start | bytes 786440 | tf_op jit(solution)/shard_map/ppermute | solution.py:28
  29.4 19.7 %collective-permute-start.8 = (bf16[1,2,64,8,128]{4,3,2,1,0:T(8,128)(2,1)S(1)}, bf16[1,2,64,8,128]{4,3,2,1,0:T(8,128)(2,1)S(1)}, u32[]{:S(2)}, u32[]{:S(2)}) collective-permute-start(bf16[1,2,64,8,128]{4,3,2,1,0:T(8,128)(2,1)S(1)} %get-tuple-element.43), channel_id=1, source_target_pairs={{0,3},{1,2},{2,1},{3,0},{4,7},{5,6},{6,5},{7,4},{8,11},{9,10},{10,... | collective-permute-start | bytes 786440 | tf_op jit(solution)/shard_map/ppermute | solution.py:28
  33.7 25.9 %collective-permute-start.5 = (bf16[2,64,8,128]{3,2,1,0:T(8,128)(2,1)S(1)}, bf16[2,64,8,128]{3,2,1,0:T(8,128)(2,1)S(1)}, u32[]{:S(2)}, u32[]{:S(2)}) collective-permute-start(bf16[2,64,8,128]{3,2,1,0:T(8,128)(2,1)S(1)} %pad_maximum_fusion), channel_id=1, source_target_pairs={{0,1},{1,0},{2,3},{3,2},{4,5},{5,4},{6,7},{7,6},{8,9},{9,8},{10,11... | collective-permute-start | bytes 786440 | tf_op jit(solution)/shard_map/ppermute | solution.py:28
  39.9 13.8 %collective-permute-start.13 = (bf16[1,64,8,128]{3,2,1,0:T(8,128)(2,1)S(1)}, bf16[1,64,8,128]{3,2,1,0:T(8,128)(2,1)S(1)}, u32[]{:S(2)}, u32[]{:S(2)}) collective-permute-start(bf16[1,64,8,128]{3,2,1,0:T(8,128)(2,1)S(1)} %get-tuple-element.51), channel_id=1, source_target_pairs={{0,3},{1,2},{2,1},{3,0},{4,7},{5,6},{6,5},{7,4},{8,11},{9,10},{10,... | collective-permute-start | bytes 393224 | tf_op jit(solution)/shard_map/ppermute | solution.py:28
  50.7 5.9 %collective-permute-start.9 = (bf16[1,64,8,128]{3,2,1,0:T(8,128)(2,1)S(1)}, bf16[1,64,8,128]{3,2,1,0:T(8,128)(2,1)S(1)}, u32[]{:S(2)}, u32[]{:S(2)}) collective-permute-start(bf16[1,64,8,128]{3,2,1,0:T(8,128)(2,1)S(1)} %get-tuple-element.45), channel_id=1, source_target_pairs={{0,3},{1,2},{2,1},{3,0},{4,7},{5,6},{6,5},{7,4},{8,11},{9,10},{10,... | collective-permute-start | bytes 393224 | tf_op jit(solution)/shard_map/ppermute | solution.py:28
  52.7 6.9 %collective-permute-start.7 = (bf16[1,64,8,128]{3,2,1,0:T(8,128)(2,1)S(1)}, bf16[1,64,8,128]{3,2,1,0:T(8,128)(2,1)S(1)}, u32[]{:S(2)}, u32[]{:S(2)}) collective-permute-start(bf16[1,64,8,128]{3,2,1,0:T(8,128)(2,1)S(1)} %get-tuple-element.42), channel_id=1, source_target_pairs={{0,2},{1,3},{2,0},{3,1},{4,6},{5,7},{6,4},{7,5},{8,10},{9,11},{10,... | collective-permute-start | bytes 393224 | tf_op jit(solution)/shard_map/ppermute | solution.py:28
  53.7 10.2 %collective-permute-start.16 = (bf16[2,256,128]{2,1,0:T(8,128)(2,1)S(1)}, bf16[2,256,128]{2,1,0:T(8,128)(2,1)S(1)}, u32[]{:S(2)}, u32[]{:S(2)}) collective-permute-start(bf16[2,256,128]{2,1,0:T(8,128)(2,1)S(1)} %get-tuple-element.56), channel_id=1, source_target_pairs={{0,24},{4,28},{8,0},{12,4},{16,8},{20,12},{24,16},{28,20},{1,25},{... | collective-permute-start | bytes 393224 | tf_op jit(solution)/shard_map/ppermute | solution.py:23
  53.7 10.2 %collective-permute-start.17 = (bf16[2,256,128]{2,1,0:T(8,128)(2,1)S(1)}, bf16[2,256,128]{2,1,0:T(8,128)(2,1)S(1)}, u32[]{:S(2)}, u32[]{:S(2)}) collective-permute-start(bf16[2,256,128]{2,1,0:T(8,128)(2,1)S(1)} %get-tuple-element.57), channel_id=1, source_target_pairs={{0,28},{4,0},{8,4},{12,8},{16,12},{20,16},{24,20},{28,24},{1,29},{... | collective-permute-start | bytes 393224 | tf_op jit(solution)/shard_map/ppermute | solution.py:23
  56.6 12.5 %collective-permute-start.14 = (bf16[2,256,128]{2,1,0:T(8,128)(2,1)S(1)}, bf16[2,256,128]{2,1,0:T(8,128)(2,1)S(1)}, u32[]{:S(2)}, u32[]{:S(2)}) collective-permute-start(bf16[2,256,128]{2,1,0:T(8,128)(2,1)S(1)} %get-tuple-element.53), channel_id=1, source_target_pairs={{0,24},{4,28},{8,0},{12,4},{16,8},{20,12},{24,16},{28,20},{1,25},{... | collective-permute-start | bytes 393224 | tf_op jit(solution)/shard_map/ppermute | solution.py:23
  59.6 9.5 %collective-permute-start.15 = (bf16[2,256,128]{2,1,0:T(8,128)(2,1)S(1)}, bf16[2,256,128]{2,1,0:T(8,128)(2,1)S(1)}, u32[]{:S(2)}, u32[]{:S(2)}) collective-permute-start(bf16[2,256,128]{2,1,0:T(8,128)(2,1)S(1)} %get-tuple-element.54), channel_id=1, source_target_pairs={{0,28},{4,0},{8,4},{12,8},{16,12},{20,16},{24,20},{28,24},{1,29},{... | collective-permute-start | bytes 393224 | tf_op jit(solution)/shard_map/ppermute | solution.py:23
  59.6 9.5 %collective-permute-start.11 = (bf16[1,64,8,128]{3,2,1,0:T(8,128)(2,1)S(1)}, bf16[1,64,8,128]{3,2,1,0:T(8,128)(2,1)S(1)}, u32[]{:S(2)}, u32[]{:S(2)}) collective-permute-start(bf16[1,64,8,128]{3,2,1,0:T(8,128)(2,1)S(1)} %get-tuple-element.48), channel_id=1, source_target_pairs={{0,2},{1,3},{2,0},{3,1},{4,6},{5,7},{6,4},{7,5},{8,10},{9,11},{10,... | collective-permute-start | bytes 393224 | tf_op jit(solution)/shard_map/ppermute | solution.py:28
